TPU v7x, 128 devices: a whole 4x4x4 slice. The times are simulated.
128 devices in a mesh: clusters: 128 (over z, y, x, core).
Axes of the slice: x: 4, y: 4, z: 4, core: 2. Of those that a mesh axis runs over, the one named last changes fastest.
Arguments:
- charges: bfloat16 [8, 524288], P(None, 'clusters'), may hold values from -6 to 6
- leaf_basis: bfloat16 [32, 524288], P(None, 'clusters'), may hold values from -0.75 to 0.75
- leaf_transfer: bfloat16 [1024, 64, 256], P('clusters'), may hold values from -0.375 to 0.375
- mid_transfer: bfloat16 [128, 64, 512], P('clusters'), may hold values from -0.25 to 0.25
- far_source: int32 [8192, 16], P('clusters'), may hold values from 0 to 8191, as said below
- far_coupling: bfloat16 [8192, 32, 512], P('clusters'), may hold values from -0.25 to 0.25
- mid_source: int32 [1024, 8], P('clusters'), may hold values from 0 to 1023, as said below
- mid_coupling: bfloat16 [1024, 64, 512], P('clusters'), may hold values from -0.25 to 0.25
- box_coupling: bfloat16 [128, 64, 192], P('clusters'), may hold values from -0.4375 to 0.4375
- top_transfer: bfloat16 [124, 64, 128], replicated, may hold values from -0.5 to 0.5
- top_coupling: bfloat16 [124, 64, 192], replicated, may hold values from -0.4375 to 0.4375
- near_target: int32 [131072], P('clusters'), may hold values from 0 to 63
- near_source: int32 [131072], P('clusters'), may hold values from 0 to 8191, as said below
- near_count: int32 [128], P('clusters'), may hold values from 256 to 1024, as said below
- near_blocks: bfloat16 [64, 8388608], P(None, 'clusters'), may hold values from -0.25 to 0.25
Outputs:
- potentials: bfloat16 [8, 524288], P(None, 'clusters')
Inputs may be any that keep to these rules, and one draw needn't show every extreme that they name: `far_source`: each source leaf lies in the row's box or in a box whose index differs by one; for each box and each box beside it, the far lists of the box's leaves name exactly 4 distinct leaves of the box beside it. `mid_source`: each source cluster lies in the row's box or in a box whose index differs by one. `near_source`: each source leaf lies in the slot's box or in a box whose index differs by one. `near_count`: slots at or after a box's count are not used.
All inputs are finite; a program needn't handle non-finite values.
Results may differ from a plain program's by a relative error of at most 0.0053.
Values may be sent and summed in bfloat16 or wider, within the bound.
No kernel may reach another device: no remote copies, remote signals or barrier semaphores. Data moves between devices by JAX's collectives and lax.ppermute only.
A program may use at most 128 MiB of HBM per device.

v0:
```python
import jax
import jax.numpy as jnp
from jax import lax
from jax.experimental import pallas as pl
from jax.experimental.pallas import tpu as pltpu
from jax.sharding import PartitionSpec as P

F32 = jnp.float32
BF16 = jnp.bfloat16

VECTORS = 8
LEAVES = 64
CAPACITY = 64
RANK_LEAF = 32
RANK = 64
GROUPS = 8
CHILDREN = 8
FAR = 16
MID_FAR = 8
SLOTS = 1024
BOXES = 128
LEVELS = 5
POINTS = LEAVES * CAPACITY
LEAF_LANES = LEAVES * RANK_LEAF
MID_LANES = GROUPS * RANK
PARTS = 8
PART = SLOTS * CAPACITY // PARTS
BLOCK = SLOTS // PARTS
WIDE = POINTS + LEAF_LANES + MID_LANES
LANES = 128
VMEM_LIMIT = 60 * 1024 * 1024


def dot_nt(left, right):
    return lax.dot_general(left, right, (((1,), (1,)), ((), ())), preferred_element_type=F32)


def dot_nn(left, right):
    return lax.dot_general(left, right, (((1,), (0,)), ((), ())), preferred_element_type=F32)


def lane_index(shape):
    return lax.broadcasted_iota(jnp.int32, shape, len(shape) - 1)


def pick_two(lane, first, second):
    return jnp.where(lane < 64, first, second)


def pick_four(lane, a, b, c, d):
    return jnp.where(lane < 64, jnp.where(lane < 32, a, b), jnp.where(lane < 96, c, d))


def up_kernel(
    charges, basis, leaf_hbm, mid_hbm, packed, message, leaf_transfer, mid_transfer, sem
):
    leaf_copy = pltpu.make_async_copy(leaf_hbm, leaf_transfer, sem.at[0])
    mid_copy = pltpu.make_async_copy(mid_hbm, mid_transfer, sem.at[1])
    leaf_copy.start()
    mid_copy.start()
    lane = lane_index((VECTORS, LANES))
    wide_lane = lane_index((VECTORS, 4 * CAPACITY)) // CAPACITY
    packed[:, pl.ds(0, POINTS)] = charges[...]
    tiles = []
    for g in range(LEAVES // 4):
        span = pl.ds(g * 4 * CAPACITY, 4 * CAPACITY)
        x = charges[:, span].astype(F32)
        rows = jnp.concatenate([jnp.where(wide_lane == j, x, 0.0) for j in range(4)], axis=0)
        b = basis[:, span]
        result = dot_nt(rows.astype(BF16), jnp.concatenate([b, b, b, b], axis=0))
        tiles.append(
            pick_four(lane, *[result[j * VECTORS : (j + 1) * VECTORS] for j in range(4)])
        )
    for g in range(LEAVES // 4):
        packed[:, pl.ds(POINTS + g * LANES, LANES)] = tiles[g].astype(BF16)
    stacked = jnp.concatenate(
        [jnp.concatenate([tiles[2 * c], tiles[2 * c + 1]], axis=1) for c in range(GROUPS)], axis=0
    ).astype(BF16)
    leaf_copy.wait()
    result = dot_nt(stacked, leaf_transfer[...].reshape(GROUPS * RANK, CHILDREN * RANK_LEAF))
    mid = []
    for h in range(GROUPS // 2):
        span = slice(h * LANES, (h + 1) * LANES)
        low = result[16 * h : 16 * h + 8, span]
        high = result[16 * h + 8 : 16 * h + 16, span]
        mid.append(pick_two(lane, low, high).astype(BF16))
        packed[:, pl.ds(POINTS + LEAF_LANES + h * LANES, LANES)] = mid[h]
    mid_copy.wait()
    box = dot_nt(jnp.concatenate(mid, axis=1), mid_transfer[0])
    box = jnp.concatenate([box, box], axis=1).astype(BF16)
    message[...] = jnp.broadcast_to(box[None], message.shape)


def side_kernel(
    near_source,
    near_target,
    near_count,
    far_source,
    mid_source,
    own,
    pair,
    other,
    far_hbm,
    mid_far_hbm,
    top_coupling_hbm,
    near_hbm,
    near_out,
    leaf_far,
    mid_far,
    coupling,
    x_low,
    x_high,
    leaf_table,
    mid_table,
    acc0,
    acc1,
    acc2,
    acc3,
    chosen_low,
    chosen_high,
    near,
    far,
    mid_coupling,
    top_coupling,
    source_rows,
    target_rows,
    far_rows,
    mid_rows,
    near_from,
    near_to,
    far_from,
    mid_from,
    near_sem,
    sem,
    index_sem,
):
    device = lax.axis_index("clusters")

    def near_copy(k):
        return pltpu.make_async_copy(
            near_hbm.at[:, pl.ds(pl.multiple_of(k * PART, PART), PART)], near.at[k], near_sem.at[k]
        )

    far_copy = pltpu.make_async_copy(far_hbm, far, sem.at[0])
    mid_copy = pltpu.make_async_copy(mid_far_hbm, mid_coupling, sem.at[1])
    top_copy = pltpu.make_async_copy(top_coupling_hbm, top_coupling, sem.at[2])
    for k in range(PARTS):
        near_copy(k).start()
    far_copy.start()
    mid_copy.start()
    top_copy.start()

    live = near_count[0]
    leaf_base = (device - 1) * LEAVES
    shape = (VECTORS, LANES)
    slot = lax.broadcasted_iota(jnp.int32, shape, 0) * LANES + lane_index(shape)
    used = slot < live
    source_rows[...] = jnp.where(used, near_source[...] - leaf_base, LEAVES) * VECTORS
    target_rows[...] = jnp.where(used, near_target[...], LEAVES) * VECTORS
    far_rows[...] = (far_source[...] - leaf_base) * VECTORS
    mid_rows[...] = (mid_source[...] - (device - 1) * GROUPS) * VECTORS
    index_copies = [
        pltpu.make_async_copy(a, b, index_sem.at[i])
        for i, (a, b) in enumerate(
            (
                (source_rows, near_from),
                (target_rows, near_to),
                (far_rows, far_from),
                (mid_rows, mid_from),
            )
        )
    ]
    for copy in index_copies:
        copy.start()

    lane = lane_index((VECTORS, LANES))
    zero = jnp.zeros((VECTORS, LANES), F32)
    odd = device % 2

    def rows_of(first):
        return pl.ds(pl.multiple_of(first, VECTORS), VECTORS)

    for source, region in ((own, 1), (pair, (1 - odd) * 2), (other, odd * 2)):
        base = region * LEAVES * VECTORS
        for h in range(LEAVES // 2):
            tile = source[:, pl.ds(h * LANES, LANES)].astype(F32)
            turned = pltpu.roll(tile, 64, 1)
            at = base + 2 * h * VECTORS
            x_low[rows_of(at), :] = pick_two(lane, tile, zero)
            x_high[rows_of(at), :] = pick_two(lane, zero, turned)
            x_low[rows_of(at + VECTORS), :] = pick_two(lane, turned, zero)
            x_high[rows_of(at + VECTORS), :] = pick_two(lane, zero, tile)
        for h in range(LEAVES // 4):
            tile = source[:, pl.ds(POINTS + h * LANES, LANES)].astype(F32)
            turns = [tile] + [pltpu.roll(tile, 32 * i, 1) for i in range(1, 4)]
            for j in range(4):
                leaf_table[rows_of(base + (4 * h + j) * VECTORS), :] = pick_four(
                    lane, *[turns[(group - j) % 4] for group in range(4)]
                )
        base = region * GROUPS * VECTORS
        for h in range(GROUPS // 2):
            tile = source[:, pl.ds(POINTS + LEAF_LANES + h * LANES, LANES)].astype(F32)
            turned = pltpu.roll(tile, 64, 1)
            at = base + 2 * h * VECTORS
            mid_table[rows_of(at), :] = pick_two(lane, tile, turned)
            mid_table[rows_of(at + VECTORS), :] = pick_two(lane, turned, tile)
    accumulators = (acc0, acc1, acc2, acc3)
    for acc in accumulators:
        acc[...] = jnp.zeros(acc.shape, F32)
    for copy in index_copies:
        copy.wait()

    zeros_half = jnp.zeros((2 * VECTORS, LANES), BF16)
    blocks = (live + BLOCK - 1) // BLOCK

    def near_step(k, carry):
        near_copy(k).wait()
        for i in range(BLOCK // 4):
            at = [rows_of(near_from[k, 4 * i + j]) for j in range(4)]
            top = jnp.concatenate([x_low[at[0], :], x_high[at[1], :]], axis=0)
            bottom = jnp.concatenate([x_low[at[2], :], x_high[at[3], :]], axis=0)
            rows = jnp.concatenate(
                [
                    jnp.concatenate([top.astype(BF16), zeros_half], axis=1),
                    jnp.concatenate([zeros_half, bottom.astype(BF16)], axis=1),
                ],
                axis=0,
            )
            result = dot_nt(rows, near[k, :, 4 * i * CAPACITY : 4 * (i + 1) * CAPACITY])
            for j in range(4):
                to = rows_of(near_to[k, 4 * i + j])
                accumulators[j][to, :] += result[j * 8 : (j + 1) * 8]
        return carry

    lax.fori_loop(0, blocks, near_step, 0)

    def unused_step(k, carry):
        near_copy(k).wait()
        return carry

    lax.fori_loop(blocks, PARTS, unused_step, 0)
    for h in range(LEAVES // 2):
        low = rows_of(2 * h * VECTORS)
        high = rows_of((2 * h + 1) * VECTORS)
        near_out[:, pl.ds(h * LANES, LANES)] = jnp.concatenate(
            [
                acc0[low, :] + acc1[low, :] + (acc2[low, :] + acc3[low, :]),
                acc0[high, :] + acc1[high, :] + (acc2[high, :] + acc3[high, :]),
            ],
            axis=1,
        )

    far_copy.wait()
    for group in range(LEAVES // 8):
        rows = []
        for i in range(8):
            leaf = group * 8 + i
            rows.append(
                jnp.concatenate(
                    [
                        pick_four(
                            lane,
                            *[leaf_table[rows_of(far_from[4 * q + m, leaf]), :] for m in range(4)],
                        )
                        for q in range(FAR // 4)
                    ],
                    axis=1,
                )
            )
        result = dot_nt(
            jnp.concatenate(rows, axis=0).astype(BF16),
            far[group * 8 : group * 8 + 8].reshape(8 * RANK_LEAF, FAR * RANK_LEAF),
        )
        for h in range(2):
            leaf_far[group * 2 + h] = pick_four(
                lane,
                *[
                    result[(4 * h + j) * 8 : (4 * h + j + 1) * 8, h * LANES : (h + 1) * LANES]
                    for j in range(4)
                ],
            )
    mid_copy.wait()
    rows = []
    for c in range(GROUPS):
        rows.append(
            jnp.concatenate(
                [
                    pick_two(
                        lane,
                        mid_table[rows_of(mid_from[c, 2 * q]), :],
                        mid_table[rows_of(mid_from[c, 2 * q + 1]), :],
                    )
                    for q in range(MID_FAR // 2)
                ],
                axis=1,
            )
        )
    result = dot_nt(
        jnp.concatenate(rows, axis=0).astype(BF16),
        mid_coupling[...].reshape(GROUPS * RANK, MID_FAR * RANK),
    )
    for h in range(GROUPS // 2):
        span = slice(h * LANES, (h + 1) * LANES)
        mid_far[h] = pick_two(
            lane, result[16 * h : 16 * h + 8, span], result[16 * h + 8 : 16 * h + 16, span]
        )

    top_copy.wait()
    tops = top_coupling.shape[2]
    level = lax.broadcasted_iota(jnp.int32, (VECTORS, tops), 0) + 1
    column = BOXES - lax.shift_right_logical(jnp.full_like(level, BOXES), level - 1)
    column = column + lax.shift_right_logical(jnp.full_like(level, 1) * device, level)
    wanted = (lane_index((VECTORS, tops)) == column).astype(F32).astype(BF16)
    for r in range(RANK):
        result = dot_nt(wanted, top_coupling[r])
        chosen_low[r * VECTORS : (r + 1) * VECTORS, :] = result[:, :LANES]
        chosen_high[r * VECTORS : (r + 1) * VECTORS, 0:RANK] = result[:, LANES:]
    for k in range(LEVELS):
        rows = pl.ds(k, RANK, stride=VECTORS)
        coupling[k, :, 0:LANES] = chosen_low[rows, :].astype(BF16)
        coupling[k, :, LANES : LANES + RANK] = chosen_high[rows, :][:, :RANK].astype(BF16)


def down_kernel(
    every,
    top_hbm,
    box_coupling,
    coupling_hbm,
    mid_hbm,
    mid_far,
    leaf_hbm,
    leaf_far,
    basis_hbm,
    near_hbm,
    out,
    top_transfer,
    coupling,
    mid_transfer,
    leaf_transfer,
    basis,
    near_field,
    sem,
    pairs0,
    pairs1,
    pairs2,
    pairs3,
    pairs4,
    pairs5,
):
    half = pl.ds(0, BOXES // 2)
    rest = pl.ds(BOXES // 2, BOXES // 2 - 4)
    copies = [
        pltpu.make_async_copy(source, target, sem.at[i])
        for i, (source, target) in enumerate(
            (
                (top_hbm.at[half], top_transfer.at[half]),
                (top_hbm.at[rest], top_transfer.at[rest]),
                (coupling_hbm, coupling),
                (mid_hbm, mid_transfer),
                (leaf_hbm, leaf_transfer),
                (basis_hbm, basis),
                (near_hbm, near_field),
            )
        )
    ]
    for copy in copies:
        copy.start()
    device = lax.axis_index("clusters")
    lane = lane_index((VECTORS, LANES))
    zero = jnp.zeros((VECTORS, LANES), F32)

    pairs = (pairs0, pairs1, pairs2, pairs3, pairs4, pairs5)
    for level in range(LEVELS + 1):
        pairs[level][0] = zero
        pairs[level][(BOXES >> (level + 1)) + 1] = zero
    for p in range(BOXES // 2):
        pairs0[p + 1] = pick_two(lane, every[2 * p].astype(F32), every[2 * p + 1].astype(F32))
    for level in range(LEVELS):
        if level < 2:
            copies[level].wait()
        start = BOXES - (BOXES >> level)
        for g in range(BOXES >> (level + 3)):
            rows = pairs[level][pl.ds(1 + 4 * g, 4)].reshape(4 * VECTORS, LANES).astype(BF16)
            matrices = top_transfer[pl.ds(start + 4 * g, 4)].reshape(4 * RANK, 2 * RANK)
            result = dot_nt(rows, matrices)
            pairs[level + 1][1 + 2 * g] = pick_two(lane, result[0:8, 0:128], result[8:16, 0:128])
            pairs[level + 1][2 + 2 * g] = pick_two(
                lane, result[16:24, 128:256], result[24:32, 128:256]
            )
    copies[2].wait()
    across = []
    for level in range(LEVELS + 1):
        cluster = device >> level
        parent = cluster >> 1
        before = pairs[level][parent]
        after = pltpu.roll(pairs[level][parent + 2], 64, 1)
        middle = jnp.where((cluster & 1) == 1, before, after)
        stacked = jnp.concatenate([pick_two(lane, before, middle), after[:, :64]], axis=1)
        matrix = box_coupling[0] if level == 0 else coupling[level - 1]
        across.append(dot_nt(stacked.astype(BF16), matrix))
    down = across[LEVELS]
    for level in range(LEVELS - 1, -1, -1):
        cluster = device >> level
        start = BOXES - (BOXES >> level)
        pushed = dot_nn(down.astype(BF16), top_transfer[start + (cluster >> 1)])
        pushed = jnp.where((cluster & 1) == 1, pltpu.roll(pushed, 64, 1), pushed)
        down = across[level] + pushed[:, :64]

    copies[3].wait()
    mid_push = dot_nn(down.astype(BF16), mid_transfer[0])
    rows = []
    for c in range(GROUPS):
        h = c // 2
        tile = mid_far[h] + mid_push[:, h * LANES : (h + 1) * LANES]
        half = pick_two(lane, tile, zero) if c % 2 == 0 else pick_two(lane, zero, tile)
        rows.append(jnp.concatenate([half if i == h else zero for i in range(GROUPS // 2)], axis=1))
    copies[4].wait()
    leaf_push = dot_nn(
        jnp.concatenate(rows, axis=0).astype(BF16),
        leaf_transfer[...].reshape(GROUPS * RANK, CHILDREN * RANK_LEAF),
    )
    copies[5].wait()
    copies[6].wait()
    lane_group = lane // RANK_LEAF
    for g in range(LEAVES // 4):
        push = leaf_push[(g // 2) * 8 : (g // 2) * 8 + 8, (g % 2) * LANES : (g % 2 + 1) * LANES]
        leaf_down = leaf_far[g] + push
        rows = jnp.concatenate(
            [jnp.where(lane_group == j, leaf_down, 0.0) for j in range(4)], axis=0
        ).astype(BF16)
        b = basis[:, pl.ds(g * 4 * CAPACITY, 4 * CAPACITY)]
        result = dot_nn(rows, jnp.concatenate([b, b, b, b], axis=0))
        for h in range(2):
            span = slice(h * LANES, (h + 1) * LANES)
            far_tile = pick_two(
                lane, result[16 * h : 16 * h + 8, span], result[16 * h + 8 : 16 * h + 16, span]
            )
            at = pl.ds((2 * g + h) * LANES, LANES)
            out[:, at] = (far_tile + near_field[:, at]).astype(BF16)


def body(
    charges,
    leaf_basis,
    leaf_transfer,
    mid_transfer,
    far_source,
    far_coupling,
    mid_source,
    mid_coupling,
    box_coupling,
    top_transfer,
    top_coupling,
    near_target,
    near_source,
    near_count,
    near_blocks,
):
    pair = [(i, i ^ 1) for i in range(BOXES)]
    other = [(i, min(max(((i + 1) ^ 1) - 1, 0), BOXES - 1)) for i in range(BOXES)]
    vmem = pl.BlockSpec(memory_space=pltpu.VMEM)
    smem = pl.BlockSpec(memory_space=pltpu.SMEM)
    hbm = pl.BlockSpec(memory_space=pltpu.HBM)
    shape = jax.ShapeDtypeStruct
    packed, message = pl.pallas_call(
        up_kernel,
        out_shape=(shape((VECTORS, WIDE), BF16), shape((BOXES, VECTORS, LANES), BF16)),
        in_specs=[vmem] * 2 + [hbm] * 2,
        out_specs=(vmem, vmem),
        scratch_shapes=[
            pltpu.VMEM((GROUPS, RANK, CHILDREN * RANK_LEAF), BF16),
            pltpu.VMEM((1, RANK, GROUPS * RANK), BF16),
            pltpu.SemaphoreType.DMA((2,)),
        ],
        cost_estimate=pl.CostEstimate(flops=10**9, bytes_accessed=10**6, transcendentals=0),
        name="upward",
    )(charges, leaf_basis, leaf_transfer, mid_transfer)
    packed_other = lax.ppermute(packed, "clusters", other)
    packed_pair = lax.ppermute(packed, "clusters", pair)
    every = lax.all_to_all(message, "clusters", 0, 0)
    table = pltpu.VMEM((3 * LEAVES * VECTORS, LANES), F32)
    accumulator = pltpu.VMEM(((LEAVES + 1) * VECTORS, CAPACITY), F32)
    near_field, leaf_far, mid_far, coupling = pl.pallas_call(
        side_kernel,
        out_shape=(
            shape((VECTORS, POINTS), F32),
            shape((LEAVES // 4, VECTORS, LANES), F32),
            shape((GROUPS // 2, VECTORS, LANES), F32),
            shape((LEVELS, RANK, 3 * RANK), BF16),
        ),
        in_specs=[vmem] * 2 + [smem] + [vmem] * 5 + [hbm] * 4,
        out_specs=(vmem,) * 4,
        scratch_shapes=[
            table,
            table,
            table,
            pltpu.VMEM((3 * GROUPS * VECTORS, LANES), F32),
            accumulator,
            accumulator,
            accumulator,
            accumulator,
            pltpu.VMEM((RANK * VECTORS, LANES), F32),
            pltpu.VMEM((RANK * VECTORS, LANES), F32),
            pltpu.VMEM((PARTS, CAPACITY, PART), BF16),
            pltpu.VMEM((LEAVES, RANK_LEAF, FAR * RANK_LEAF), BF16),
            pltpu.VMEM((GROUPS, RANK, MID_FAR * RANK), BF16),
            pltpu.VMEM((RANK, 3 * RANK, BOXES - 4), BF16),
            pltpu.VMEM((VECTORS, LANES), jnp.int32),
            pltpu.VMEM((VECTORS, LANES), jnp.int32),
            pltpu.VMEM((FAR, LEAVES), jnp.int32),
            pltpu.VMEM((GROUPS, MID_FAR), jnp.int32),
            pltpu.SMEM((VECTORS, LANES), jnp.int32),
            pltpu.SMEM((VECTORS, LANES), jnp.int32),
            pltpu.SMEM((FAR, LEAVES), jnp.int32),
            pltpu.SMEM((GROUPS, MID_FAR), jnp.int32),
            pltpu.SemaphoreType.DMA((PARTS,)),
            pltpu.SemaphoreType.DMA((3,)),
            pltpu.SemaphoreType.DMA((4,)),
        ],
        cost_estimate=pl.CostEstimate(flops=2 * 10**9, bytes_accessed=10**7, transcendentals=0),
        compiler_params=pltpu.CompilerParams(vmem_limit_bytes=VMEM_LIMIT),
        name="side",
    )(
        near_source.reshape(VECTORS, LANES),
        near_target.reshape(VECTORS, LANES),
        near_count,
        far_source.T,
        mid_source,
        packed,
        packed_pair,
        packed_other,
        far_coupling,
        mid_coupling,
        jnp.transpose(top_coupling, (1, 2, 0)),
        near_blocks,
    )
    return pl.pallas_call(
        down_kernel,
        out_shape=shape((VECTORS, POINTS), BF16),
        in_specs=[vmem, hbm, vmem, hbm, hbm, vmem, hbm, vmem, hbm, hbm],
        out_specs=vmem,
        scratch_shapes=[
            pltpu.VMEM((BOXES - 4, RANK, 2 * RANK), BF16),
            pltpu.VMEM((LEVELS, RANK, 3 * RANK), BF16),
            pltpu.VMEM((1, RANK, GROUPS * RANK), BF16),
            pltpu.VMEM((GROUPS, RANK, CHILDREN * RANK_LEAF), BF16),
            pltpu.VMEM((RANK_LEAF, POINTS), BF16),
            pltpu.VMEM((VECTORS, POINTS), F32),
            pltpu.SemaphoreType.DMA((7,)),
        ]
        + [
            pltpu.VMEM(((BOXES >> (level + 1)) + 2, VECTORS, LANES), F32)
            for level in range(LEVELS + 1)
        ],
        cost_estimate=pl.CostEstimate(flops=10**9, bytes_accessed=10**6, transcendentals=0),
        name="down",
    )(
        every,
        top_transfer,
        box_coupling,
        coupling,
        mid_transfer,
        mid_far,
        leaf_transfer,
        leaf_far,
        leaf_basis,
        near_field,
    )


def solution(mesh):
    in_specs = (
        P(None, "clusters"),
        P(None, "clusters"),
        P("clusters", None, None),
        P("clusters", None, None),
        P("clusters", None),
        P("clusters", None, None),
        P("clusters", None),
        P("clusters", None, None),
        P("clusters", None, None),
        P(),
        P(),
        P("clusters"),
        P("clusters"),
        P("clusters"),
        P(None, "clusters"),
    )
    out_specs = P(None, "clusters")
    return jax.shard_map(body, mesh=mesh, in_specs=in_specs, out_specs=out_specs, check_vma=False)
```

profile of v0, /device:TPU:1, one launch (start us, length us, event | category | flops | bytes accessed | tf_op | source)
XLA Modules:
  0.0 35.6 jit_solution(9565908594724553132)
XLA Ops:
  0.0 3.1 %upward.1 = (bf16[8,6656]{1,0:T(8,128)(2,1)}, bf16[128,8,128]{2,1,0:T(8,128)(2,1)}) custom-call(bf16[8,4096]{1,0:T(8,128)(2,1)} %charges.1, bf16[32,4096]{1,0:T(8,128)(2,1)} %basis_hbm.1, bf16[8,64,256]{2,1,0:T(8,128)(2,1)} %leaf_hbm.3, bf16[1,64,512]{2,1,0:T(8,128)(2,1)} %mid_hbm.3), custom_call_target="tpu_custom_call" | custom-call | flops 1000000000 | bytes 1000000 | tf_op jit(solution)/shard_map/upward/pallas_call | solution.py:465
  3.1 4.5 %collective-permute-start.1 = (bf16[8,6656]{1,0:T(8,128)(2,1)}, bf16[8,6656]{1,0:T(8,128)(2,1)S(1)}, u32[]{:S(2)}, u32[]{:S(2)}) collective-permute-start(bf16[8,6656]{1,0:T(8,128)(2,1)} %get-tuple-element.12.own), channel_id=1, source_target_pairs={{0,0},{1,2},{2,1},{3,4},{4,3},{5,6},{6,5},{7,8},{8,7},{9,10},{10,9... | collective-permute-start | bytes 319496 | tf_op jit(solution)/shard_map/ppermute | solution.py:478
  7.6 0.1 collective-permute-start
  7.7 10.2 %all-to-all-start = ((bf16[128,8,128]{2,1,0:T(8,128)(2,1)}), bf16[128,8,128]{2,1,0:T(8,128)(2,1)S(1)}, u32[]{:S(2)}, u32[]{:S(2)}) async-start(bf16[128,8,128]{2,1,0:T(8,128)(2,1)} %get-tuple-element.11), calls=%async_computation | async-start | bytes 524288 | tf_op jit(solution)/shard_map/all_to_all | solution.py:480
  18.5 0.0 collective-permute-done.1.other
  18.5 0.0 copy-start.1
  18.6 0.0 collective-permute-done.pair
  18.6 0.0 copy-start.2
  18.6 0.6 %copy-done.1 = bf16[8,6656]{1,0:T(8,128)(2,1)} copy-done((bf16[8,6656]{1,0:T(8,128)(2,1)}, bf16[8,6656]{1,0:T(8,128)(2,1)S(1)}, u32[]{:S(2)}) %copy-start.1) | copy-done | bytes 106520
  19.2 0.0 copy-done.2
  19.2 9.9 %side.1 = (f32[8,4096]{1,0:T(8,128)}, f32[16,8,128]{2,1,0:T(8,128)}, f32[4,8,128]{2,1,0:T(8,128)}, bf16[5,64,192]{2,1,0:T(8,128)(2,1)}) custom-call(s32[8,128]{1,0:T(8,128)} %bitcast.6, s32[8,128]{1,0:T(8,128)} %bitcast.7, s32[1]{0:T(128)S(6)} %copy.16.near_count, s32[16,64]{1,0:T(8,128)} %bitcast.5, s32[8,8]{1,0:T(8,128)} %mid_source.1, ...), custom_call_target="tpu_custom_call" | custom-call | flops 2000000000 | bytes 10000000 | tf_op jit(solution)/shard_map/side/pallas_call | solution.py:483
  29.2 0.0 all-to-all-done.every
  29.2 0.0 copy-start
  29.2 0.7 %copy-done = bf16[128,8,128]{2,1,0:T(8,128)(2,1)} copy-done((bf16[128,8,128]{2,1,0:T(8,128)(2,1)}, bf16[128,8,128]{2,1,0:T(8,128)(2,1)S(1)}, u32[]{:S(2)}) %copy-start) | copy-done | bytes 262168
  29.9 5.7 %down.1 = bf16[8,4096]{1,0:T(8,128)(2,1)} custom-call(bf16[128,8,128]{2,1,0:T(8,128)(2,1)} %copy-done, bf16[124,64,128]{2,1,0:T(8,128)(2,1)} %top_hbm.1, bf16[1,64,192]{2,1,0:T(8,128)(2,1)} %box_coupling.1, bf16[5,64,192]{2,1,0:T(8,128)(2,1)} %get-tuple-element.13.coupling_hbm, bf16[1,64,512]{2,1,0:T(8,128)(2,1)} %mid_hbm.3, ...), custom_call_target="tpu_custom_call" | custom-call | flops 1000000000 | bytes 1000000 | tf_op jit(solution)/shard_map/down/pallas_call | solution.py:537
Async XLA Ops:
  3.1 15.4 %collective-permute-start.1 = (bf16[8,6656]{1,0:T(8,128)(2,1)}, bf16[8,6656]{1,0:T(8,128)(2,1)S(1)}, u32[]{:S(2)}, u32[]{:S(2)}) collective-permute-start(bf16[8,6656]{1,0:T(8,128)(2,1)} %get-tuple-element.12.own), channel_id=1, source_target_pairs={{0,0},{1,2},{2,1},{3,4},{4,3},{5,6},{6,5},{7,8},{8,7},{9,10},{10,9... | collective-permute-start | bytes 319496 | tf_op jit(solution)/shard_map/ppermute | solution.py:478
  7.6 11.0 %collective-permute-start = (bf16[8,6656]{1,0:T(8,128)(2,1)}, bf16[8,6656]{1,0:T(8,128)(2,1)S(1)}, u32[]{:S(2)}, u32[]{:S(2)}) collective-permute-start(bf16[8,6656]{1,0:T(8,128)(2,1)} %get-tuple-element.12.own), channel_id=1, source_target_pairs={{0,1},{1,0},{2,3},{3,2},{4,5},{5,4},{6,7},{7,6},{8,9},{9,8},{10,11... | collective-permute-start | bytes 319496 | tf_op jit(solution)/shard_map/ppermute | solution.py:479
  7.7 21.5 %all-to-all-start = ((bf16[128,8,128]{2,1,0:T(8,128)(2,1)}), bf16[128,8,128]{2,1,0:T(8,128)(2,1)S(1)}, u32[]{:S(2)}, u32[]{:S(2)}) async-start(bf16[128,8,128]{2,1,0:T(8,128)(2,1)} %get-tuple-element.11), calls=%async_computation | async-start | bytes 524288 | tf_op jit(solution)/shard_map/all_to_all | solution.py:480
  18.5 0.7 %copy-start.1 = (bf16[8,6656]{1,0:T(8,128)(2,1)}, bf16[8,6656]{1,0:T(8,128)(2,1)S(1)}, u32[]{:S(2)}) copy-start(bf16[8,6656]{1,0:T(8,128)(2,1)S(1)} %collective-permute-done.1.other) | copy-start | bytes 319492
  18.6 0.7 %copy-start.2 = (bf16[8,6656]{1,0:T(8,128)(2,1)}, bf16[8,6656]{1,0:T(8,128)(2,1)S(1)}, u32[]{:S(2)}) copy-start(bf16[8,6656]{1,0:T(8,128)(2,1)S(1)} %collective-permute-done.pair) | copy-start | bytes 319492
  29.2 0.7 %copy-start = (bf16[128,8,128]{2,1,0:T(8,128)(2,1)}, bf16[128,8,128]{2,1,0:T(8,128)(2,1)S(1)}, u32[]{:S(2)}) copy-start(bf16[128,8,128]{2,1,0:T(8,128)(2,1)S(1)} %all-to-all-done.every) | copy-start | bytes 786436
where the time goes:
time: 35.9 us; the launch traced here: 35.6 us
  Pallas kernels  18.7 us (52%)
  starting transfers between devices  14.8 us (41%)
  local copies, waits for them, and re-layouts  1.35 us (4%)
  between operations  0.74 us (2%)
    all_to_all x1, starting transfers between devices, body(): every = lax.all_to_all(message, 'clusters', 0, 0)  10.2 us
    pallas_call x1, Pallas kernels, body(): pl.pallas_call(side_kernel, out_shape=(shape((VECTORS, POINTS), F32), sha...  9.93 us
    pallas_call x1, Pallas kernels, body(): pl.pallas_call(down_kernel, out_shape=shape((VECTORS, POINTS), BF16), in_...  5.74 us
    ppermute x1, starting transfers between devices, body(): packed_other = lax.ppermute(packed, 'clusters', other)  4.5 us
    pallas_call x1, Pallas kernels, body(): pl.pallas_call(up_kernel, out_shape=(shape((VECTORS, WIDE), BF16), shape(...  3.08 us
    unnamed x6, local copies, waits for them, and re-layouts  1.35 us
  transfers between devices with their start and end apart: 3, of which 0 were waited for; matrix products, arithmetic and copies ran while one was open for 0% of the time, Pallas kernels for 28%

commit v1 on v0

v1 whole, which is shorter than its diff:
```python
import jax
import jax.numpy as jnp
from jax import lax
from jax.experimental import pallas as pl
from jax.experimental.pallas import tpu as pltpu
from jax.sharding import PartitionSpec as P

F32 = jnp.float32
BF16 = jnp.bfloat16

VECTORS = 8
LEAVES = 64
CAPACITY = 64
RANK_LEAF = 32
RANK = 64
GROUPS = 8
CHILDREN = 8
FAR = 16
MID_FAR = 8
SLOTS = 1024
BOXES = 128
LEVELS = 5
POINTS = LEAVES * CAPACITY
LEAF_LANES = LEAVES * RANK_LEAF
MID_LANES = GROUPS * RANK
PARTS = 8
PART = SLOTS * CAPACITY // PARTS
BLOCK = SLOTS // PARTS
WIDE = POINTS + LEAF_LANES + MID_LANES
LANES = 128
VMEM_LIMIT = 60 * 1024 * 1024
MESSAGES = 16
LEAF_AT = LEAVES // 2
MID_AT = LEAF_AT + LEAVES // 4
FIELDS = MID_AT + GROUPS // 2


def dot_nt(left, right):
    return lax.dot_general(left, right, (((1,), (1,)), ((), ())), preferred_element_type=F32)


def dot_nn(left, right):
    return lax.dot_general(left, right, (((1,), (0,)), ((), ())), preferred_element_type=F32)


def lane_index(shape):
    return lax.broadcasted_iota(jnp.int32, shape, len(shape) - 1)


def pick_two(lane, first, second):
    return jnp.where(lane < 64, first, second)


def pick_four(lane, a, b, c, d):
    return jnp.where(lane < 64, jnp.where(lane < 32, a, b), jnp.where(lane < 96, c, d))


def rows_of(first):
    return pl.ds(pl.multiple_of(first, VECTORS), VECTORS)


def up_kernel(
    charges_hbm,
    basis_hbm,
    leaf_hbm,
    mid_hbm,
    packed_hbm,
    message_hbm,
    charges,
    basis,
    leaf_transfer,
    mid_transfer,
    coefficients,
    message,
    sem,
    out_sem,
):
    copies = [
        pltpu.make_async_copy(a, b, sem.at[i])
        for i, (a, b) in enumerate(
            (
                (charges_hbm, charges),
                (basis_hbm, basis),
                (leaf_hbm, leaf_transfer),
                (mid_hbm, mid_transfer),
            )
        )
    ]
    for copy in copies:
        copy.start()
    lane = lane_index((VECTORS, LANES))
    wide_lane = lane_index((VECTORS, 4 * CAPACITY)) // CAPACITY
    copies[0].wait()
    charges_out = pltpu.make_async_copy(
        charges, packed_hbm.at[:, pl.ds(0, POINTS)], out_sem.at[0]
    )
    charges_out.start()
    copies[1].wait()
    tiles = []
    for g in range(LEAVES // 4):
        span = pl.ds(g * 4 * CAPACITY, 4 * CAPACITY)
        x = charges[:, span].astype(F32)
        rows = jnp.concatenate([jnp.where(wide_lane == j, x, 0.0) for j in range(4)], axis=0)
        result = dot_nt(rows.astype(BF16), basis[:, span])
        tiles.append(
            jnp.concatenate([result[j * VECTORS : (j + 1) * VECTORS] for j in range(4)], axis=1)
        )
    for g in range(LEAVES // 4):
        coefficients[:, pl.ds(g * LANES, LANES)] = tiles[g].astype(BF16)
    stacked = jnp.concatenate(
        [jnp.concatenate([tiles[2 * c], tiles[2 * c + 1]], axis=1) for c in range(GROUPS)], axis=0
    ).astype(BF16)
    copies[2].wait()
    result = dot_nt(stacked, leaf_transfer[...].reshape(GROUPS * RANK, CHILDREN * RANK_LEAF))
    mid = []
    for h in range(GROUPS // 2):
        span = slice(h * LANES, (h + 1) * LANES)
        low = result[16 * h : 16 * h + 8, span]
        high = result[16 * h + 8 : 16 * h + 16, span]
        mid.append(pick_two(lane, low, high).astype(BF16))
        coefficients[:, pl.ds(LEAF_LANES + h * LANES, LANES)] = mid[h]
    coefficients_out = pltpu.make_async_copy(
        coefficients, packed_hbm.at[:, pl.ds(POINTS, LEAF_LANES + MID_LANES)], out_sem.at[1]
    )
    coefficients_out.start()
    copies[3].wait()
    box = dot_nt(jnp.concatenate(mid, axis=1), mid_transfer[0])
    box = jnp.concatenate([box, box], axis=1).astype(BF16)
    message[...] = jnp.broadcast_to(box[None], message.shape)
    messages_out = [
        pltpu.make_async_copy(
            message, message_hbm.at[pl.ds(i * MESSAGES, MESSAGES)], out_sem.at[2 + i]
        )
        for i in range(BOXES // MESSAGES)
    ]
    for copy in messages_out:
        copy.start()
    charges_out.wait()
    coefficients_out.wait()
    for copy in messages_out:
        copy.wait()


def side_kernel(
    near_source_hbm,
    near_target_hbm,
    near_count_hbm,
    far_source_hbm,
    mid_source_hbm,
    own_hbm,
    pair_hbm,
    other_hbm,
    far_hbm,
    mid_far_hbm,
    top_coupling_hbm,
    top_transfer_hbm,
    box_coupling_hbm,
    near_hbm,
    field_hbm,
    coupling_hbm,
    near_source,
    near_target,
    far_source,
    mid_source,
    own,
    pair,
    other,
    far,
    mid_coupling,
    top_coupling,
    parents,
    box_coupling,
    near,
    field,
    coupling,
    x_low,
    x_high,
    leaf_table,
    mid_table,
    acc0,
    acc1,
    acc2,
    acc3,
    chosen_low,
    chosen_high,
    source_rows,
    target_rows,
    far_rows,
    mid_rows,
    near_count,
    near_from,
    near_to,
    far_from,
    mid_from,
    near_sem,
    sem,
    parent_sem,
    index_sem,
    out_sem,
):
    device = lax.axis_index("clusters")

    def near_copy(k):
        return pltpu.make_async_copy(
            near_hbm.at[:, pl.ds(pl.multiple_of(k * PART, PART), PART)], near.at[k], near_sem.at[k]
        )

    copies = [
        pltpu.make_async_copy(a, b, sem.at[i])
        for i, (a, b) in enumerate(
            (
                (near_count_hbm, near_count),
                (near_source_hbm, near_source),
                (near_target_hbm, near_target),
                (far_source_hbm, far_source),
                (mid_source_hbm, mid_source),
                (own_hbm, own),
                (pair_hbm, pair),
                (other_hbm, other),
                (box_coupling_hbm, box_coupling),
                (far_hbm, far),
                (mid_far_hbm, mid_coupling),
                (top_coupling_hbm, top_coupling),
            )
        )
    ]
    parent_copies = []
    for level in range(LEVELS):
        start = BOXES - (BOXES >> level)
        parent_copies.append(
            pltpu.make_async_copy(
                top_transfer_hbm.at[start + (device >> (level + 1))],
                parents.at[level],
                parent_sem.at[level],
            )
        )
    for copy in copies[:8]:
        copy.start()
    near_copy(0).start()
    near_copy(1).start()
    for copy in parent_copies:
        copy.start()
    copies[8].start()

    for copy in copies[:5]:
        copy.wait()
    live = near_count[0, 0]
    leaf_base = (device - 1) * LEAVES
    shape = (VECTORS, LANES)
    slot = lax.broadcasted_iota(jnp.int32, shape, 0) * LANES + lane_index(shape)
    used = slot < live
    source_rows[...] = jnp.where(used, near_source[...] - leaf_base, LEAVES) * VECTORS
    target_rows[...] = jnp.where(used, near_target[...], LEAVES) * VECTORS
    far_rows[...] = (far_source[...] - leaf_base) * VECTORS
    mid_rows[...] = (mid_source[...] - (device - 1) * GROUPS) * VECTORS
    index_copies = [
        pltpu.make_async_copy(a, b, index_sem.at[i])
        for i, (a, b) in enumerate(
            (
                (source_rows, near_from),
                (target_rows, near_to),
                (far_rows, far_from),
                (mid_rows, mid_from),
            )
        )
    ]
    for copy in index_copies:
        copy.start()
    blocks = jnp.clip((live + BLOCK - 1) // BLOCK, 2, PARTS)
    for k in (2, 3):

        @pl.when(k < blocks)
        def _(k=k):
            near_copy(k).start()

    lane = lane_index((VECTORS, LANES))
    zero = jnp.zeros((VECTORS, LANES), F32)
    odd = device % 2
    accumulators = (acc0, acc1, acc2, acc3)
    for acc in accumulators:
        acc[...] = jnp.zeros(acc.shape, F32)
    for copy in copies[5:8]:
        copy.wait()
    for source, region in ((own, 1), (pair, (1 - odd) * 2), (other, odd * 2)):
        base = region * LEAVES * VECTORS
        for h in range(LEAVES // 2):
            tile = source[:, pl.ds(h * LANES, LANES)].astype(F32)
            turned = pltpu.roll(tile, 64, 1)
            at = base + 2 * h * VECTORS
            x_low[rows_of(at), :] = pick_two(lane, tile, zero)
            x_high[rows_of(at), :] = pick_two(lane, zero, turned)
            x_low[rows_of(at + VECTORS), :] = pick_two(lane, turned, zero)
            x_high[rows_of(at + VECTORS), :] = pick_two(lane, zero, tile)
        for h in range(LEAVES // 4):
            tile = source[:, pl.ds(POINTS + h * LANES, LANES)].astype(F32)
            turns = [tile] + [pltpu.roll(tile, 32 * i, 1) for i in range(1, 4)]
            for j in range(4):
                leaf_table[rows_of(base + (4 * h + j) * VECTORS), :] = pick_four(
                    lane, *[turns[(group - j) % 4] for group in range(4)]
                )
        base = region * GROUPS * VECTORS
        for h in range(GROUPS // 2):
            tile = source[:, pl.ds(POINTS + LEAF_LANES + h * LANES, LANES)].astype(F32)
            turned = pltpu.roll(tile, 64, 1)
            at = base + 2 * h * VECTORS
            mid_table[rows_of(at), :] = pick_two(lane, tile, turned)
            mid_table[rows_of(at + VECTORS), :] = pick_two(lane, turned, tile)
    for copy in index_copies:
        copy.wait()

    zeros_half = jnp.zeros((2 * VECTORS, LANES), BF16)

    def near_step(k, carry):
        @pl.when(k + 4 < blocks)
        def _():
            near_copy(k + 4).start()

        @pl.when(k == 0)
        def _():
            copies[9].start()
            copies[10].start()

        @pl.when(k == 1)
        def _():
            copies[11].start()

        near_copy(k).wait()
        for i in range(BLOCK // 4):
            at = [rows_of(near_from[k, 4 * i + j]) for j in range(4)]
            top = jnp.concatenate([x_low[at[0], :], x_high[at[1], :]], axis=0)
            bottom = jnp.concatenate([x_low[at[2], :], x_high[at[3], :]], axis=0)
            rows = jnp.concatenate(
                [
                    jnp.concatenate([top.astype(BF16), zeros_half], axis=1),
                    jnp.concatenate([zeros_half, bottom.astype(BF16)], axis=1),
                ],
                axis=0,
            )
            result = dot_nt(rows, near[k, :, 4 * i * CAPACITY : 4 * (i + 1) * CAPACITY])
            for j in range(4):
                to = rows_of(near_to[k, 4 * i + j])
                accumulators[j][to, :] += result[j * 8 : (j + 1) * 8]
        return carry

    lax.fori_loop(0, blocks, near_step, 0)
    for h in range(LEAVES // 2):
        low = rows_of(2 * h * VECTORS)
        high = rows_of((2 * h + 1) * VECTORS)
        field[h] = jnp.concatenate(
            [
                acc0[low, :] + acc1[low, :] + (acc2[low, :] + acc3[low, :]),
                acc0[high, :] + acc1[high, :] + (acc2[high, :] + acc3[high, :]),
            ],
            axis=1,
        )

    for copy in parent_copies:
        copy.wait()
    square = (RANK, RANK)
    product = (
        lax.broadcasted_iota(jnp.int32, square, 0) == lax.broadcasted_iota(jnp.int32, square, 1)
    ).astype(F32)
    products = []
    for level in range(LEVELS):
        parent = parents[level].astype(F32)
        own_half = jnp.where(
            ((device >> level) & 1) == 1, pltpu.roll(parent, RANK, 1), parent
        )[:, :RANK]
        product = dot_nt(product.astype(BF16), own_half.astype(BF16))
        products.append(product.astype(BF16))

    copies[9].wait()
    for group in range(LEAVES // 8):
        rows = []
        for i in range(8):
            leaf = group * 8 + i
            rows.append(
                jnp.concatenate(
                    [
                        pick_four(
                            lane,
                            *[leaf_table[rows_of(far_from[4 * q + m, leaf]), :] for m in range(4)],
                        )
                        for q in range(FAR // 4)
                    ],
                    axis=1,
                )
            )
        result = dot_nt(
            jnp.concatenate(rows, axis=0).astype(BF16),
            far[group * 8 : group * 8 + 8].reshape(8 * RANK_LEAF, FAR * RANK_LEAF),
        )
        for h in range(2):
            field[LEAF_AT + group * 2 + h] = pick_four(
                lane,
                *[
                    result[(4 * h + j) * 8 : (4 * h + j + 1) * 8, h * LANES : (h + 1) * LANES]
                    for j in range(4)
                ],
            )
    copies[10].wait()
    rows = []
    for c in range(GROUPS):
        rows.append(
            jnp.concatenate(
                [
                    pick_two(
                        lane,
                        mid_table[rows_of(mid_from[c, 2 * q]), :],
                        mid_table[rows_of(mid_from[c, 2 * q + 1]), :],
                    )
                    for q in range(MID_FAR // 2)
                ],
                axis=1,
            )
        )
    result = dot_nt(
        jnp.concatenate(rows, axis=0).astype(BF16),
        mid_coupling[...].reshape(GROUPS * RANK, MID_FAR * RANK),
    )
    for h in range(GROUPS // 2):
        span = slice(h * LANES, (h + 1) * LANES)
        field[MID_AT + h] = pick_two(
            lane, result[16 * h : 16 * h + 8, span], result[16 * h + 8 : 16 * h + 16, span]
        )
    field_out = pltpu.make_async_copy(field, field_hbm, out_sem.at[0])
    field_out.start()

    copies[11].wait()
    tops = top_coupling.shape[2]
    level = lax.broadcasted_iota(jnp.int32, (VECTORS, tops), 0) + 1
    column = BOXES - lax.shift_right_logical(jnp.full_like(level, BOXES), level - 1)
    column = column + lax.shift_right_logical(jnp.full_like(level, 1) * device, level)
    wanted = (lane_index((VECTORS, tops)) == column).astype(F32).astype(BF16)
    for r in range(RANK):
        result = dot_nt(wanted, top_coupling[r])
        chosen_low[r * VECTORS : (r + 1) * VECTORS, :] = result[:, :LANES]
        chosen_high[r * VECTORS : (r + 1) * VECTORS, 0:RANK] = result[:, LANES:]
    copies[8].wait()
    coupling[0] = box_coupling[0]
    for k in range(LEVELS):
        rows = pl.ds(k, RANK, stride=VECTORS)
        chosen = jnp.concatenate([chosen_low[rows, :], chosen_high[rows, :][:, :RANK]], axis=1)
        coupling[k + 1] = dot_nn(products[k], chosen.astype(BF16)).astype(BF16)
    coupling_out = pltpu.make_async_copy(coupling, coupling_hbm, out_sem.at[1])
    coupling_out.start()
    field_out.wait()
    coupling_out.wait()


def down_kernel(
    every_hbm,
    top_hbm,
    coupling_hbm,
    mid_hbm,
    leaf_hbm,
    field_hbm,
    basis_hbm,
    out,
    every,
    top_transfer,
    coupling,
    mid_transfer,
    leaf_transfer,
    field,
    basis,
    sem,
    pairs0,
    pairs1,
    pairs2,
    pairs3,
    pairs4,
    pairs5,
):
    half = pl.ds(0, BOXES // 2)
    rest = pl.ds(BOXES // 2, BOXES // 2 - 4)
    copies = [
        pltpu.make_async_copy(source, target, sem.at[i])
        for i, (source, target) in enumerate(
            (
                (every_hbm, every),
                (top_hbm.at[half], top_transfer.at[half]),
                (top_hbm.at[rest], top_transfer.at[rest]),
                (coupling_hbm, coupling),
                (mid_hbm, mid_transfer),
                (leaf_hbm, leaf_transfer),
                (field_hbm, field),
                (basis_hbm, basis),
            )
        )
    ]
    for copy in copies:
        copy.start()
    device = lax.axis_index("clusters")
    lane = lane_index((VECTORS, LANES))
    zero = jnp.zeros((VECTORS, LANES), F32)
    empty = jnp.zeros((2 * VECTORS, LANES), BF16)

    pairs = (pairs0, pairs1, pairs2, pairs3, pairs4, pairs5)
    for level in range(LEVELS + 1):
        pairs[level][0] = zero
        pairs[level][(BOXES >> (level + 1)) + 1] = zero
    copies[0].wait()
    for p in range(BOXES // 2):
        pairs0[p + 1] = pick_two(lane, every[2 * p].astype(F32), every[2 * p + 1].astype(F32))
    for level in range(LEVELS):
        if level < 2:
            copies[1 + level].wait()
        start = BOXES - (BOXES >> level)
        count = BOXES >> (level + 1)
        for g in range(0, count, 8):
            left, right = [], []
            for quad in range(g, min(g + 8, count), 4):
                low = jnp.concatenate([pairs[level][1 + quad], pairs[level][2 + quad]], axis=0)
                high = jnp.concatenate([pairs[level][3 + quad], pairs[level][4 + quad]], axis=0)
                left.append(jnp.concatenate([low.astype(BF16), empty], axis=1))
                left.append(jnp.concatenate([empty, high.astype(BF16)], axis=1))
                at = start + quad
                right.append(jnp.concatenate([top_transfer[at], top_transfer[at + 2]], axis=1))
                right.append(jnp.concatenate([top_transfer[at + 1], top_transfer[at + 3]], axis=1))
            result = dot_nt(jnp.concatenate(left, axis=0), jnp.concatenate(right, axis=0))
            for i in range(len(left)):
                span = slice((i // 2) * LANES, (i // 2 + 1) * LANES)
                pairs[level + 1][1 + g // 2 + i] = pick_two(
                    lane, result[16 * i : 16 * i + 8, span], result[16 * i + 8 : 16 * i + 16, span]
                )
    copies[3].wait()
    down = jnp.zeros((VECTORS, RANK), F32)
    for level in range(LEVELS + 1):
        cluster = device >> level
        parent = cluster >> 1
        before = pairs[level][parent]
        after = pltpu.roll(pairs[level][parent + 2], 64, 1)
        middle = jnp.where((cluster & 1) == 1, before, after)
        stacked = jnp.concatenate([pick_two(lane, before, middle), after[:, :64]], axis=1)
        down = down + dot_nt(stacked.astype(BF16), coupling[level])

    copies[4].wait()
    mid_push = dot_nn(down.astype(BF16), mid_transfer[0])
    copies[5].wait()
    copies[6].wait()
    rows = []
    for c in range(GROUPS):
        h = c // 2
        tile = field[MID_AT + h] + mid_push[:, h * LANES : (h + 1) * LANES]
        half_tile = pick_two(lane, tile, zero) if c % 2 == 0 else pick_two(lane, zero, tile)
        rows.append(
            jnp.concatenate([half_tile if i == h else zero for i in range(GROUPS // 2)], axis=1)
        )
    leaf_push = dot_nn(
        jnp.concatenate(rows, axis=0).astype(BF16),
        leaf_transfer[...].reshape(GROUPS * RANK, CHILDREN * RANK_LEAF),
    )
    copies[7].wait()
    lane_group = lane // RANK_LEAF
    for g in range(LEAVES // 4):
        push = leaf_push[(g // 2) * 8 : (g // 2) * 8 + 8, (g % 2) * LANES : (g % 2 + 1) * LANES]
        leaf_down = field[LEAF_AT + g] + push
        rows = jnp.concatenate(
            [jnp.where(lane_group == j, leaf_down, 0.0) for j in range(4)], axis=0
        ).astype(BF16)
        b = basis[:, pl.ds(g * 4 * CAPACITY, 4 * CAPACITY)]
        result = dot_nn(rows, jnp.concatenate([b, b, b, b], axis=0))
        for h in range(2):
            span = slice(h * LANES, (h + 1) * LANES)
            far_tile = pick_two(
                lane, result[16 * h : 16 * h + 8, span], result[16 * h + 8 : 16 * h + 16, span]
            )
            out[:, pl.ds((2 * g + h) * LANES, LANES)] = (far_tile + field[2 * g + h]).astype(BF16)


def body(
    charges,
    leaf_basis,
    leaf_transfer,
    mid_transfer,
    far_source,
    far_coupling,
    mid_source,
    mid_coupling,
    box_coupling,
    top_transfer,
    top_coupling,
    near_target,
    near_source,
    near_count,
    near_blocks,
):
    pair = [(i, i ^ 1) for i in range(BOXES)]
    other = [(i, min(max(((i + 1) ^ 1) - 1, 0), BOXES - 1)) for i in range(BOXES)]
    vmem = pl.BlockSpec(memory_space=pltpu.VMEM)
    hbm = pl.BlockSpec(memory_space=pltpu.HBM)
    shape = jax.ShapeDtypeStruct
    scratch = pltpu.VMEM
    dma = pltpu.SemaphoreType.DMA
    packed, message = pl.pallas_call(
        up_kernel,
        out_shape=(shape((VECTORS, WIDE), BF16), shape((BOXES, VECTORS, LANES), BF16)),
        in_specs=[hbm] * 4,
        out_specs=(hbm, hbm),
        scratch_shapes=[
            scratch((VECTORS, POINTS), BF16),
            scratch((RANK_LEAF, POINTS), BF16),
            scratch((GROUPS, RANK, CHILDREN * RANK_LEAF), BF16),
            scratch((1, RANK, GROUPS * RANK), BF16),
            scratch((VECTORS, LEAF_LANES + MID_LANES), BF16),
            scratch((MESSAGES, VECTORS, LANES), BF16),
            dma((4,)),
            dma((2 + BOXES // MESSAGES,)),
        ],
        cost_estimate=pl.CostEstimate(flops=10**9, bytes_accessed=10**6, transcendentals=0),
        compiler_params=pltpu.CompilerParams(vmem_limit_bytes=VMEM_LIMIT),
        name="upward",
    )(charges, leaf_basis, leaf_transfer, mid_transfer)
    packed_other = lax.ppermute(packed, "clusters", other)
    packed_pair = lax.ppermute(packed, "clusters", pair)
    every = lax.all_to_all(message, "clusters", 0, 0)
    table = scratch((3 * LEAVES * VECTORS, LANES), F32)
    accumulator = scratch(((LEAVES + 1) * VECTORS, CAPACITY), F32)
    indices = [
        (VECTORS, LANES),
        (VECTORS, LANES),
        (FAR, LEAVES),
        (GROUPS, MID_FAR),
    ]
    wide = scratch((VECTORS, WIDE), BF16)
    field, coupling = pl.pallas_call(
        side_kernel,
        out_shape=(
            shape((FIELDS, VECTORS, LANES), F32),
            shape((LEVELS + 1, RANK, 3 * RANK), BF16),
        ),
        in_specs=[hbm] * 14,
        out_specs=(hbm, hbm),
        scratch_shapes=[scratch(i, jnp.int32) for i in indices]
        + [
            wide,
            wide,
            wide,
            scratch((LEAVES, RANK_LEAF, FAR * RANK_LEAF), BF16),
            scratch((GROUPS, RANK, MID_FAR * RANK), BF16),
            scratch((RANK, 3 * RANK, BOXES - 4), BF16),
            scratch((LEVELS, RANK, 2 * RANK), BF16),
            scratch((1, RANK, 3 * RANK), BF16),
            scratch((PARTS, CAPACITY, PART), BF16),
            scratch((FIELDS, VECTORS, LANES), F32),
            scratch((LEVELS + 1, RANK, 3 * RANK), BF16),
            table,
            table,
            table,
            scratch((3 * GROUPS * VECTORS, LANES), F32),
            accumulator,
            accumulator,
            accumulator,
            accumulator,
            scratch((RANK * VECTORS, LANES), F32),
            scratch((RANK * VECTORS, LANES), F32),
        ]
        + [scratch(i, jnp.int32) for i in indices]
        + [pltpu.SMEM((1, 1), jnp.int32)]
        + [pltpu.SMEM(i, jnp.int32) for i in indices]
        + [dma((PARTS,)), dma((12,)), dma((LEVELS,)), dma((4,)), dma((2,))],
        cost_estimate=pl.CostEstimate(flops=2 * 10**9, bytes_accessed=10**7, transcendentals=0),
        compiler_params=pltpu.CompilerParams(vmem_limit_bytes=VMEM_LIMIT),
        name="side",
    )(
        near_source.reshape(VECTORS, LANES),
        near_target.reshape(VECTORS, LANES),
        near_count.reshape(1, 1),
        far_source.T,
        mid_source,
        packed,
        packed_pair,
        packed_other,
        far_coupling,
        mid_coupling,
        jnp.transpose(top_coupling, (1, 2, 0)),
        top_transfer,
        box_coupling,
        near_blocks,
    )
    return pl.pallas_call(
        down_kernel,
        out_shape=shape((VECTORS, POINTS), BF16),
        in_specs=[hbm] * 7,
        out_specs=vmem,
        scratch_shapes=[
            scratch((BOXES, VECTORS, LANES), BF16),
            scratch((BOXES - 4, RANK, 2 * RANK), BF16),
            scratch((LEVELS + 1, RANK, 3 * RANK), BF16),
            scratch((1, RANK, GROUPS * RANK), BF16),
            scratch((GROUPS, RANK, CHILDREN * RANK_LEAF), BF16),
            scratch((FIELDS, VECTORS, LANES), F32),
            scratch((RANK_LEAF, POINTS), BF16),
            dma((8,)),
        ]
        + [
            scratch(((BOXES >> (level + 1)) + 2, VECTORS, LANES), F32)
            for level in range(LEVELS + 1)
        ],
        cost_estimate=pl.CostEstimate(flops=10**9, bytes_accessed=10**6, transcendentals=0),
        compiler_params=pltpu.CompilerParams(vmem_limit_bytes=VMEM_LIMIT),
        name="down",
    )(every, top_transfer, coupling, mid_transfer, leaf_transfer, field, leaf_basis)


def solution(mesh):
    in_specs = (
        P(None, "clusters"),
        P(None, "clusters"),
        P("clusters", None, None),
        P("clusters", None, None),
        P("clusters", None),
        P("clusters", None, None),
        P("clusters", None),
        P("clusters", None, None),
        P("clusters", None, None),
        P(),
        P(),
        P("clusters"),
        P("clusters"),
        P("clusters"),
        P(None, "clusters"),
    )
    out_specs = P(None, "clusters")
    return jax.shard_map(body, mesh=mesh, in_specs=in_specs, out_specs=out_specs, check_vma=False)
```

time: 35.9 us -> 33.3 us (0.928)
  Pallas kernels: 18.7 us -> 14.3 us
  waiting for transfers between devices: 0.01 us -> 1.94 us
    pallas_call x1, Pallas kernels: 9.93 us -> 7.76 us  [body(): pl.pallas_call(side_kernel, out_shape=(shape((FIELDS, VECTORS, LANES), F3...]
    all_to_all x1, waiting for transfers between devices: 0.01 us -> 1.94 us  [body(): every = lax.all_to_all(message, 'clusters', 0, 0)]
    pallas_call x1, Pallas kernels: 5.74 us -> 4.01 us  [body(): pl.pallas_call(down_kernel, out_shape=shape((VECTORS, POINTS), BF16), in_...]
    pallas_call x1, Pallas kernels: 3.08 us -> 2.49 us  [body(): pl.pallas_call(up_kernel, out_shape=(shape((VECTORS, WIDE), BF16), shape(...]
  transfers between devices with their start and end apart: 3 -> 3, of which waited for: 0 -> 1; matrix products, arithmetic and copies ran while one was open for 0% -> 0% of each run, Pallas kernels for 28% -> 23%
where the time goes in v1:
time: 33.3 us; the launch traced here: 33.1 us
  starting transfers between devices  14.8 us (44%)
  Pallas kernels  14.3 us (43%)
  waiting for transfers between devices  1.94 us (6%)
  local copies, waits for them, and re-layouts  1.37 us (4%)
  between operations  0.72 us (2%)
    all_to_all x1, starting transfers between devices, body(): every = lax.all_to_all(message, 'clusters', 0, 0)  10.2 us
    pallas_call x1, Pallas kernels, body(): pl.pallas_call(side_kernel, out_shape=(shape((FIELDS, VECTORS, LANES), F3...  7.76 us
    ppermute x1, starting transfers between devices, body(): packed_other = lax.ppermute(packed, 'clusters', other)  4.5 us
    pallas_call x1, Pallas kernels, body(): pl.pallas_call(down_kernel, out_shape=shape((VECTORS, POINTS), BF16), in_...  4.01 us
    pallas_call x1, Pallas kernels, body(): pl.pallas_call(up_kernel, out_shape=(shape((VECTORS, WIDE), BF16), shape(...  2.49 us
    all_to_all x1, waiting for transfers between devices, body(): every = lax.all_to_all(message, 'clusters', 0, 0)  1.94 us
    unnamed x6, local copies, waits for them, and re-layouts  1.37 us
  transfers between devices with their start and end apart: 3, of which 1 were waited for; matrix products, arithmetic and copies ran while one was open for 0% of the time, Pallas kernels for 23%

profile of v1, /device:TPU:1, one launch (start us, length us, event | category | flops | bytes accessed | tf_op | source)
XLA Modules:
  0.0 33.1 jit_solution(4871700402844755655)
XLA Ops:
  0.0 2.5 %upward.1 = (bf16[8,6656]{1,0:T(8,128)(2,1)}, bf16[128,8,128]{2,1,0:T(8,128)(2,1)}) custom-call(bf16[8,4096]{1,0:T(8,128)(2,1)} %charges_hbm.1, bf16[32,4096]{1,0:T(8,128)(2,1)} %basis_hbm.3, bf16[8,64,256]{2,1,0:T(8,128)(2,1)} %leaf_hbm.3, bf16[1,64,512]{2,1,0:T(8,128)(2,1)} %mid_hbm.3), custom_call_target="tpu_custom_call" | custom-call | flops 1000000000 | bytes 1000000 | tf_op jit(solution)/shard_map/upward/pallas_call | solution.py:596
  2.5 4.5 %collective-permute-start.1 = (bf16[8,6656]{1,0:T(8,128)(2,1)}, bf16[8,6656]{1,0:T(8,128)(2,1)S(1)}, u32[]{:S(2)}, u32[]{:S(2)}) collective-permute-start(bf16[8,6656]{1,0:T(8,128)(2,1)} %get-tuple-element.10.own_hbm), channel_id=1, source_target_pairs={{0,0},{1,2},{2,1},{3,4},{4,3},{5,6},{6,5},{7,8},{8,7},{9,10},{10,9... | collective-permute-start | bytes 319496 | tf_op jit(solution)/shard_map/ppermute | solution.py:615
  7.0 0.1 collective-permute-start
  7.1 10.2 %all-to-all-start = ((bf16[128,8,128]{2,1,0:T(8,128)(2,1)}), bf16[128,8,128]{2,1,0:T(8,128)(2,1)S(1)}, u32[]{:S(2)}, u32[]{:S(2)}) async-start(bf16[128,8,128]{2,1,0:T(8,128)(2,1)} %get-tuple-element.9), calls=%async_computation | async-start | bytes 524288 | tf_op jit(solution)/shard_map/all_to_all | solution.py:617
  17.9 0.0 collective-permute-done.1.other_hbm
  18.0 0.0 copy-start.1
  18.0 0.0 collective-permute-done.pair_hbm
  18.0 0.0 copy-start.2
  18.0 0.6 %copy-done.1 = bf16[8,6656]{1,0:T(8,128)(2,1)} copy-done((bf16[8,6656]{1,0:T(8,128)(2,1)}, bf16[8,6656]{1,0:T(8,128)(2,1)S(1)}, u32[]{:S(2)}) %copy-start.1) | copy-done | bytes 106520
  18.6 0.1 copy-done.2
  18.7 7.8 %side.1 = (f32[52,8,128]{2,1,0:T(8,128)}, bf16[6,64,192]{2,1,0:T(8,128)(2,1)}) custom-call(s32[8,128]{1,0:T(8,128)} %bitcast.8, s32[8,128]{1,0:T(8,128)} %bitcast.9, s32[1,1]{1,0:T(1,128)} %bitcast.5.near_count_hbm, s32[16,64]{1,0:T(8,128)} %bitcast.7, s32[8,8]{1,0:T(8,128)} %mid_source_hbm.1, bf16[8,6656]{1,0:T(8,128)(2,1)} %get-tuple-element.10.own_hbm, ...), custom_call_target="tpu_custom_call" | custom-call | flops 2000000000 | bytes 10000000 | tf_op jit(solution)/shard_map/side/pallas_call | solution.py:627
  26.4 1.9 %all-to-all-done.every_hbm = bf16[128,8,128]{2,1,0:T(8,128)(2,1)S(1)} async-done(((bf16[128,8,128]{2,1,0:T(8,128)(2,1)}), bf16[128,8,128]{2,1,0:T(8,128)(2,1)S(1)}, u32[]{:S(2)}, u32[]{:S(2)}) %all-to-all-start) | async-done | bytes 262176 | tf_op jit(solution)/shard_map/all_to_all | solution.py:617
  28.4 0.0 copy-start
  28.4 0.7 %copy-done = bf16[128,8,128]{2,1,0:T(8,128)(2,1)} copy-done((bf16[128,8,128]{2,1,0:T(8,128)(2,1)}, bf16[128,8,128]{2,1,0:T(8,128)(2,1)S(1)}, u32[]{:S(2)}) %copy-start) | copy-done | bytes 262168
  29.1 4.0 %down.1 = bf16[8,4096]{1,0:T(8,128)(2,1)} custom-call(bf16[128,8,128]{2,1,0:T(8,128)(2,1)} %copy-done, bf16[124,64,128]{2,1,0:T(8,128)(2,1)} %top_hbm.1, bf16[6,64,192]{2,1,0:T(8,128)(2,1)} %get-tuple-element.11.coupling_hbm, bf16[1,64,512]{2,1,0:T(8,128)(2,1)} %mid_hbm.3, bf16[8,64,256]{2,1,0:T(8,128)(2,1)} %leaf_hbm.3, ...), custom_call_target="tpu_custom_call" | custom-call | flops 1000000000 | bytes 1000000 | tf_op jit(solution)/shard_map/down/pallas_call | solution.py:682
Async XLA Ops:
  2.5 15.4 %collective-permute-start.1 = (bf16[8,6656]{1,0:T(8,128)(2,1)}, bf16[8,6656]{1,0:T(8,128)(2,1)S(1)}, u32[]{:S(2)}, u32[]{:S(2)}) collective-permute-start(bf16[8,6656]{1,0:T(8,128)(2,1)} %get-tuple-element.10.own_hbm), channel_id=1, source_target_pairs={{0,0},{1,2},{2,1},{3,4},{4,3},{5,6},{6,5},{7,8},{8,7},{9,10},{10,9... | collective-permute-start | bytes 319496 | tf_op jit(solution)/shard_map/ppermute | solution.py:615
  7.0 11.0 %collective-permute-start = (bf16[8,6656]{1,0:T(8,128)(2,1)}, bf16[8,6656]{1,0:T(8,128)(2,1)S(1)}, u32[]{:S(2)}, u32[]{:S(2)}) collective-permute-start(bf16[8,6656]{1,0:T(8,128)(2,1)} %get-tuple-element.10.own_hbm), channel_id=1, source_target_pairs={{0,1},{1,0},{2,3},{3,2},{4,5},{5,4},{6,7},{7,6},{8,9},{9,8},{10,11... | collective-permute-start | bytes 319496 | tf_op jit(solution)/shard_map/ppermute | solution.py:616
  7.1 21.3 %all-to-all-start = ((bf16[128,8,128]{2,1,0:T(8,128)(2,1)}), bf16[128,8,128]{2,1,0:T(8,128)(2,1)S(1)}, u32[]{:S(2)}, u32[]{:S(2)}) async-start(bf16[128,8,128]{2,1,0:T(8,128)(2,1)} %get-tuple-element.9), calls=%async_computation | async-start | bytes 524288 | tf_op jit(solution)/shard_map/all_to_all | solution.py:617
  18.0 0.6 %copy-start.1 = (bf16[8,6656]{1,0:T(8,128)(2,1)}, bf16[8,6656]{1,0:T(8,128)(2,1)S(1)}, u32[]{:S(2)}) copy-start(bf16[8,6656]{1,0:T(8,128)(2,1)S(1)} %collective-permute-done.1.other_hbm) | copy-start | bytes 319492
  18.0 0.7 %copy-start.2 = (bf16[8,6656]{1,0:T(8,128)(2,1)}, bf16[8,6656]{1,0:T(8,128)(2,1)S(1)}, u32[]{:S(2)}) copy-start(bf16[8,6656]{1,0:T(8,128)(2,1)S(1)} %collective-permute-done.pair_hbm) | copy-start | bytes 319492
  28.4 0.7 %copy-start = (bf16[128,8,128]{2,1,0:T(8,128)(2,1)}, bf16[128,8,128]{2,1,0:T(8,128)(2,1)S(1)}, u32[]{:S(2)}) copy-start(bf16[128,8,128]{2,1,0:T(8,128)(2,1)S(1)} %all-to-all-done.every_hbm) | copy-start | bytes 786436

commit v2 on v1

--- a/solution.py
+++ b/solution.py
@@ -55,6 +55,10 @@
     return jnp.where(lane < 64, jnp.where(lane < 32, a, b), jnp.where(lane < 96, c, d))
 
 
+def turn(tile, groups):
+    return tile if groups % 4 == 0 else pltpu.roll(tile, RANK_LEAF * (groups % 4), 1)
+
+
 def rows_of(first):
     return pl.ds(pl.multiple_of(first, VECTORS), VECTORS)
 
@@ -97,14 +101,21 @@
     charges_out.start()
     copies[1].wait()
     tiles = []
-    for g in range(LEAVES // 4):
-        span = pl.ds(g * 4 * CAPACITY, 4 * CAPACITY)
-        x = charges[:, span].astype(F32)
-        rows = jnp.concatenate([jnp.where(wide_lane == j, x, 0.0) for j in range(4)], axis=0)
-        result = dot_nt(rows.astype(BF16), basis[:, span])
-        tiles.append(
-            jnp.concatenate([result[j * VECTORS : (j + 1) * VECTORS] for j in range(4)], axis=1)
-        )
+    for first in range(0, LEAVES // 4, 8):
+        rows, weights = [], []
+        for g in range(first, first + 8):
+            span = pl.ds(g * 4 * CAPACITY, 4 * CAPACITY)
+            x = charges[:, span].astype(F32)
+            rows += [jnp.where(wide_lane == j, x, 0.0) for j in range(4)]
+            weights.append(basis[:, span])
+        result = dot_nt(
+            jnp.concatenate(rows, axis=0).astype(BF16), jnp.concatenate(weights, axis=0)
+        )
+        for g in range(8):
+            tile = result[32 * g : 32 * (g + 1), (g // 4) * LANES : (g // 4 + 1) * LANES]
+            tiles.append(
+                pick_four(lane, *[turn(tile[8 * j : 8 * (j + 1)], j - g % 4) for j in range(4)])
+            )
     for g in range(LEAVES // 4):
         coefficients[:, pl.ds(g * LANES, LANES)] = tiles[g].astype(BF16)
     stacked = jnp.concatenate(
@@ -125,13 +136,14 @@
     coefficients_out.start()
     copies[3].wait()
     box = dot_nt(jnp.concatenate(mid, axis=1), mid_transfer[0])
-    box = jnp.concatenate([box, box], axis=1).astype(BF16)
+    box = jnp.concatenate([box[:4], box[4:]], axis=1)
+    box = jnp.concatenate([box, box], axis=0).astype(BF16)
     message[...] = jnp.broadcast_to(box[None], message.shape)
     messages_out = [
         pltpu.make_async_copy(
             message, message_hbm.at[pl.ds(i * MESSAGES, MESSAGES)], out_sem.at[2 + i]
         )
-        for i in range(BOXES // MESSAGES)
+        for i in range(BOXES // 2 // MESSAGES)
     ]
     for copy in messages_out:
         copy.start()
@@ -325,34 +337,33 @@
             copies[11].start()
 
         near_copy(k).wait()
-        for i in range(BLOCK // 4):
-            at = [rows_of(near_from[k, 4 * i + j]) for j in range(4)]
-            top = jnp.concatenate([x_low[at[0], :], x_high[at[1], :]], axis=0)
-            bottom = jnp.concatenate([x_low[at[2], :], x_high[at[3], :]], axis=0)
-            rows = jnp.concatenate(
-                [
-                    jnp.concatenate([top.astype(BF16), zeros_half], axis=1),
-                    jnp.concatenate([zeros_half, bottom.astype(BF16)], axis=1),
-                ],
-                axis=0,
-            )
-            result = dot_nt(rows, near[k, :, 4 * i * CAPACITY : 4 * (i + 1) * CAPACITY])
-            for j in range(4):
-                to = rows_of(near_to[k, 4 * i + j])
-                accumulators[j][to, :] += result[j * 8 : (j + 1) * 8]
+        for i in range(BLOCK // 16):
+            rows, weights = [], []
+            for g in range(4):
+                first = 16 * i + 4 * g
+                at = [rows_of(near_from[k, first + j]) for j in range(4)]
+                top = jnp.concatenate([x_low[at[0], :], x_high[at[1], :]], axis=0)
+                bottom = jnp.concatenate([x_low[at[2], :], x_high[at[3], :]], axis=0)
+                rows.append(jnp.concatenate([top.astype(BF16), zeros_half], axis=1))
+                rows.append(jnp.concatenate([zeros_half, bottom.astype(BF16)], axis=1))
+                weights.append(near[k, :, first * CAPACITY : (first + 4) * CAPACITY])
+            result = dot_nt(jnp.concatenate(rows, axis=0), jnp.concatenate(weights, axis=0))
+            for g in range(4):
+                for j in range(4):
+                    to = rows_of(near_to[k, 16 * i + 4 * g + j])
+                    at = 32 * g + 8 * j
+                    accumulators[g][to, :] += result[
+                        at : at + 8, (g // 2) * LANES : (g // 2 + 1) * LANES
+                    ]
         return carry
 
     lax.fori_loop(0, blocks, near_step, 0)
     for h in range(LEAVES // 2):
         low = rows_of(2 * h * VECTORS)
         high = rows_of((2 * h + 1) * VECTORS)
-        field[h] = jnp.concatenate(
-            [
-                acc0[low, :] + acc1[low, :] + (acc2[low, :] + acc3[low, :]),
-                acc0[high, :] + acc1[high, :] + (acc2[high, :] + acc3[high, :]),
-            ],
-            axis=1,
-        )
+        placed = pick_two(lane, acc0[low, :] + acc2[low, :], acc1[high, :] + acc3[high, :])
+        moved = pick_two(lane, acc0[high, :] + acc2[high, :], acc1[low, :] + acc3[low, :])
+        field[h] = placed + pltpu.roll(moved, CAPACITY, 1)
 
     for copy in parent_copies:
         copy.wait()
@@ -501,8 +512,10 @@
         pairs[level][0] = zero
         pairs[level][(BOXES >> (level + 1)) + 1] = zero
     copies[0].wait()
+    kept = (lane < RANK) == (lax.broadcasted_iota(jnp.int32, (VECTORS, LANES), 0) < 4)
     for p in range(BOXES // 2):
-        pairs0[p + 1] = pick_two(lane, every[2 * p].astype(F32), every[2 * p + 1].astype(F32))
+        tile = every[p].astype(F32)
+        pairs0[p + 1] = jnp.where(kept, tile, pltpu.roll(pltpu.roll(tile, RANK, 1), 4, 0))
     for level in range(LEVELS):
         if level < 2:
             copies[1 + level].wait()
@@ -553,20 +566,28 @@
     )
     copies[7].wait()
     lane_group = lane // RANK_LEAF
-    for g in range(LEAVES // 4):
-        push = leaf_push[(g // 2) * 8 : (g // 2) * 8 + 8, (g % 2) * LANES : (g % 2 + 1) * LANES]
-        leaf_down = field[LEAF_AT + g] + push
-        rows = jnp.concatenate(
-            [jnp.where(lane_group == j, leaf_down, 0.0) for j in range(4)], axis=0
-        ).astype(BF16)
-        b = basis[:, pl.ds(g * 4 * CAPACITY, 4 * CAPACITY)]
-        result = dot_nn(rows, jnp.concatenate([b, b, b, b], axis=0))
-        for h in range(2):
-            span = slice(h * LANES, (h + 1) * LANES)
-            far_tile = pick_two(
-                lane, result[16 * h : 16 * h + 8, span], result[16 * h + 8 : 16 * h + 16, span]
-            )
-            out[:, pl.ds((2 * g + h) * LANES, LANES)] = (far_tile + field[2 * g + h]).astype(BF16)
+    for first in range(0, LEAVES // 4, 8):
+        rows, weights = [], []
+        for g in range(first, first + 8):
+            push = leaf_push[(g // 2) * 8 : (g // 2) * 8 + 8, (g % 2) * LANES : (g % 2 + 1) * LANES]
+            leaf_down = field[LEAF_AT + g] + push
+            for j in range(4):
+                block = jnp.where(lane_group == g % 4, turn(leaf_down, g % 4 - j), 0.0)
+                rows.append(
+                    jnp.concatenate([block, zero] if g % 8 < 4 else [zero, block], axis=1)
+                )
+            weights.append(basis[:, pl.ds(g * 4 * CAPACITY, 4 * CAPACITY)])
+        result = dot_nn(
+            jnp.concatenate(rows, axis=0).astype(BF16), jnp.concatenate(weights, axis=0)
+        )
+        for g in range(first, first + 8):
+            for h in range(2):
+                span = slice(h * LANES, (h + 1) * LANES)
+                at = 32 * (g % 8) + 16 * h
+                far_tile = pick_two(lane, result[at : at + 8, span], result[at + 8 : at + 16, span])
+                out[:, pl.ds((2 * g + h) * LANES, LANES)] = (far_tile + field[2 * g + h]).astype(
+                    BF16
+                )
 
 
 def body(
@@ -595,7 +616,7 @@
     dma = pltpu.SemaphoreType.DMA
     packed, message = pl.pallas_call(
         up_kernel,
-        out_shape=(shape((VECTORS, WIDE), BF16), shape((BOXES, VECTORS, LANES), BF16)),
+        out_shape=(shape((VECTORS, WIDE), BF16), shape((BOXES // 2, VECTORS, LANES), BF16)),
         in_specs=[hbm] * 4,
         out_specs=(hbm, hbm),
         scratch_shapes=[
@@ -606,7 +627,7 @@
             scratch((VECTORS, LEAF_LANES + MID_LANES), BF16),
             scratch((MESSAGES, VECTORS, LANES), BF16),
             dma((4,)),
-            dma((2 + BOXES // MESSAGES,)),
+            dma((2 + BOXES // 2 // MESSAGES,)),
         ],
         cost_estimate=pl.CostEstimate(flops=10**9, bytes_accessed=10**6, transcendentals=0),
         compiler_params=pltpu.CompilerParams(vmem_limit_bytes=VMEM_LIMIT),
@@ -614,9 +635,9 @@
     )(charges, leaf_basis, leaf_transfer, mid_transfer)
     packed_other = lax.ppermute(packed, "clusters", other)
     packed_pair = lax.ppermute(packed, "clusters", pair)
-    every = lax.all_to_all(message, "clusters", 0, 0)
+    every = lax.all_to_all(message.reshape(BOXES, VECTORS // 2, LANES), "clusters", 0, 0)
     table = scratch((3 * LEAVES * VECTORS, LANES), F32)
-    accumulator = scratch(((LEAVES + 1) * VECTORS, CAPACITY), F32)
+    accumulator = scratch(((LEAVES + 1) * VECTORS, LANES), F32)
     indices = [
         (VECTORS, LANES),
         (VECTORS, LANES),
@@ -685,7 +706,7 @@
         in_specs=[hbm] * 7,
         out_specs=vmem,
         scratch_shapes=[
-            scratch((BOXES, VECTORS, LANES), BF16),
+            scratch((BOXES // 2, VECTORS, LANES), BF16),
             scratch((BOXES - 4, RANK, 2 * RANK), BF16),
             scratch((LEVELS + 1, RANK, 3 * RANK), BF16),
             scratch((1, RANK, GROUPS * RANK), BF16),
@@ -701,7 +722,7 @@
         cost_estimate=pl.CostEstimate(flops=10**9, bytes_accessed=10**6, transcendentals=0),
         compiler_params=pltpu.CompilerParams(vmem_limit_bytes=VMEM_LIMIT),
         name="down",
-    )(every, top_transfer, coupling, mid_transfer, leaf_transfer, field, leaf_basis)
+    )(every.reshape(BOXES // 2, VECTORS, LANES), top_transfer, coupling, mid_transfer, leaf_transfer, field, leaf_basis)
 
 
 def solution(mesh):

time: 33.3 us -> 33.2 us (level)
  the two profiles are of different devices: /device:TPU:1 before, /device:TPU:127 now
where the time goes in v2:
time: 33.2 us; the launch traced here: 33 us
  Pallas kernels  17.7 us (53%)
  starting transfers between devices  13.3 us (40%)
  local copies, waits for them, and re-layouts  1.31 us (4%)
  between operations  0.72 us (2%)
    pallas_call x1, Pallas kernels, body(): pl.pallas_call(side_kernel, out_shape=(shape((FIELDS, VECTORS, LANES), F3...  11.2 us
    all_to_all x1, starting transfers between devices, body(): lax.all_to_all(message.reshape(BOXES, VECTORS // 2, LANES), 'clusters', 0...  10.3 us
    pallas_call x1, Pallas kernels, body(): pl.pallas_call(down_kernel, out_shape=shape((VECTORS, POINTS), BF16), in_...  3.98 us
    pallas_call x1, Pallas kernels, body(): pl.pallas_call(up_kernel, out_shape=(shape((VECTORS, WIDE), BF16), shape(...  2.48 us
    ppermute x1, starting transfers between devices, body(): packed_other = lax.ppermute(packed, 'clusters', other)  1.55 us
    ppermute x1, starting transfers between devices, body(): packed_pair = lax.ppermute(packed, 'clusters', pair)  1.39 us
    unnamed x6, local copies, waits for them, and re-layouts  1.31 us
  transfers between devices with their start and end apart: 3, of which 0 were waited for; matrix products, arithmetic and copies ran while one was open for 0% of the time, Pallas kernels for 34%

profile of v2, /device:TPU:127, one launch (start us, length us, event | category | flops | bytes accessed | tf_op | source)
XLA Modules:
  0.0 33.0 jit_solution(5862706145512846050)
XLA Ops:
  0.0 2.5 %upward.1 = (bf16[8,6656]{1,0:T(8,128)(2,1)}, bf16[64,8,128]{2,1,0:T(8,128)(2,1)}) custom-call(bf16[8,4096]{1,0:T(8,128)(2,1)} %charges_hbm.1, bf16[32,4096]{1,0:T(8,128)(2,1)} %basis_hbm.3, bf16[8,64,256]{2,1,0:T(8,128)(2,1)} %leaf_hbm.3, bf16[1,64,512]{2,1,0:T(8,128)(2,1)} %mid_hbm.3), custom_call_target="tpu_custom_call" | custom-call | flops 1000000000 | bytes 1000000 | tf_op jit(solution)/shard_map/upward/pallas_call | solution.py:617
  2.5 1.6 %collective-permute-start.1 = (bf16[8,6656]{1,0:T(8,128)(2,1)}, bf16[8,6656]{1,0:T(8,128)(2,1)S(1)}, u32[]{:S(2)}, u32[]{:S(2)}) collective-permute-start(bf16[8,6656]{1,0:T(8,128)(2,1)} %get-tuple-element.10.own_hbm), channel_id=1, source_target_pairs={{0,0},{1,2},{2,1},{3,4},{4,3},{5,6},{6,5},{7,8},{8,7},{9,10},{10,9... | collective-permute-start | bytes 319496 | tf_op jit(solution)/shard_map/ppermute | solution.py:636
  4.0 1.4 %collective-permute-start = (bf16[8,6656]{1,0:T(8,128)(2,1)}, bf16[8,6656]{1,0:T(8,128)(2,1)S(1)}, u32[]{:S(2)}, u32[]{:S(2)}) collective-permute-start(bf16[8,6656]{1,0:T(8,128)(2,1)} %get-tuple-element.10.own_hbm), channel_id=1, source_target_pairs={{0,1},{1,0},{2,3},{3,2},{4,5},{5,4},{6,7},{7,6},{8,9},{9,8},{10,11... | collective-permute-start | bytes 319496 | tf_op jit(solution)/shard_map/ppermute | solution.py:637
  5.4 10.3 %all-to-all-start = ((bf16[128,4,128]{2,1,0:T(4,128)(2,1)}), bf16[128,4,128]{2,1,0:T(4,128)(2,1)S(1)}, u32[]{:S(2)}, u32[]{:S(2)}) async-start(bf16[128,4,128]{2,1,0:T(4,128)(2,1)} %bitcast.9), calls=%async_computation | async-start | bytes 262144 | tf_op jit(solution)/shard_map/all_to_all | solution.py:638
  16.4 0.0 collective-permute-done.1.other_hbm
  16.4 0.0 copy-start.1
  16.4 0.0 collective-permute-done.pair_hbm
  16.5 0.0 copy-start.2
  16.5 0.6 %copy-done.1 = bf16[8,6656]{1,0:T(8,128)(2,1)} copy-done((bf16[8,6656]{1,0:T(8,128)(2,1)}, bf16[8,6656]{1,0:T(8,128)(2,1)S(1)}, u32[]{:S(2)}) %copy-start.1) | copy-done | bytes 106520
  17.1 0.0 copy-done.2
  17.1 11.2 %side.1 = (f32[52,8,128]{2,1,0:T(8,128)}, bf16[6,64,192]{2,1,0:T(8,128)(2,1)}) custom-call(s32[8,128]{1,0:T(8,128)} %bitcast.12, s32[8,128]{1,0:T(8,128)} %bitcast.13, s32[1,1]{1,0:T(1,128)} %bitcast.7.near_count_hbm, s32[16,64]{1,0:T(8,128)} %bitcast.11, s32[8,8]{1,0:T(8,128)} %mid_source_hbm.1, bf16[8,6656]{1,0:T(8,128)(2,1)} %get-tuple-element.10.own_hbm, ...), custom_call_target="tpu_custom_call" | custom-call | flops 2000000000 | bytes 10000000 | tf_op jit(solution)/shard_map/side/pallas_call | solution.py:648
  28.3 0.0 all-to-all-done
  28.3 0.0 copy-start
  28.4 0.6 %copy-done = bf16[128,4,128]{2,1,0:T(4,128)(2,1)} copy-done((bf16[128,4,128]{2,1,0:T(4,128)(2,1)}, bf16[128,4,128]{2,1,0:T(4,128)(2,1)S(1)}, u32[]{:S(2)}) %copy-start) | copy-done | bytes 131096
  29.0 4.0 %down.1 = bf16[8,4096]{1,0:T(8,128)(2,1)} custom-call(bf16[64,8,128]{2,1,0:T(8,128)(2,1)} %bitcast.10, bf16[124,64,128]{2,1,0:T(8,128)(2,1)} %top_hbm.1, bf16[6,64,192]{2,1,0:T(8,128)(2,1)} %get-tuple-element.11.coupling_hbm, bf16[1,64,512]{2,1,0:T(8,128)(2,1)} %mid_hbm.3, bf16[8,64,256]{2,1,0:T(8,128)(2,1)} %leaf_hbm.3, ...), custom_call_target="tpu_custom_call" | custom-call | flops 1000000000 | bytes 1000000 | tf_op jit(solution)/shard_map/down/pallas_call | solution.py:703
Async XLA Ops:
  2.5 13.9 %collective-permute-start.1 = (bf16[8,6656]{1,0:T(8,128)(2,1)}, bf16[8,6656]{1,0:T(8,128)(2,1)S(1)}, u32[]{:S(2)}, u32[]{:S(2)}) collective-permute-start(bf16[8,6656]{1,0:T(8,128)(2,1)} %get-tuple-element.10.own_hbm), channel_id=1, source_target_pairs={{0,0},{1,2},{2,1},{3,4},{4,3},{5,6},{6,5},{7,8},{8,7},{9,10},{10,9... | collective-permute-start | bytes 319496 | tf_op jit(solution)/shard_map/ppermute | solution.py:636
  4.0 12.4 %collective-permute-start = (bf16[8,6656]{1,0:T(8,128)(2,1)}, bf16[8,6656]{1,0:T(8,128)(2,1)S(1)}, u32[]{:S(2)}, u32[]{:S(2)}) collective-permute-start(bf16[8,6656]{1,0:T(8,128)(2,1)} %get-tuple-element.10.own_hbm), channel_id=1, source_target_pairs={{0,1},{1,0},{2,3},{3,2},{4,5},{5,4},{6,7},{7,6},{8,9},{9,8},{10,11... | collective-permute-start | bytes 319496 | tf_op jit(solution)/shard_map/ppermute | solution.py:637
  5.4 22.9 %all-to-all-start = ((bf16[128,4,128]{2,1,0:T(4,128)(2,1)}), bf16[128,4,128]{2,1,0:T(4,128)(2,1)S(1)}, u32[]{:S(2)}, u32[]{:S(2)}) async-start(bf16[128,4,128]{2,1,0:T(4,128)(2,1)} %bitcast.9), calls=%async_computation | async-start | bytes 262144 | tf_op jit(solution)/shard_map/all_to_all | solution.py:638
  16.4 0.6 %copy-start.1 = (bf16[8,6656]{1,0:T(8,128)(2,1)}, bf16[8,6656]{1,0:T(8,128)(2,1)S(1)}, u32[]{:S(2)}) copy-start(bf16[8,6656]{1,0:T(8,128)(2,1)S(1)} %collective-permute-done.1.other_hbm) | copy-start | bytes 319492
  16.5 0.7 %copy-start.2 = (bf16[8,6656]{1,0:T(8,128)(2,1)}, bf16[8,6656]{1,0:T(8,128)(2,1)S(1)}, u32[]{:S(2)}) copy-start(bf16[8,6656]{1,0:T(8,128)(2,1)S(1)} %collective-permute-done.pair_hbm) | copy-start | bytes 319492
  28.3 0.7 %copy-start = (bf16[128,4,128]{2,1,0:T(4,128)(2,1)}, bf16[128,4,128]{2,1,0:T(4,128)(2,1)S(1)}, u32[]{:S(2)}) copy-start(bf16[128,4,128]{2,1,0:T(4,128)(2,1)S(1)} %all-to-all-done) | copy-start | bytes 393220

commit v3 on v2

--- a/solution.py
+++ b/solution.py
@@ -23,16 +23,22 @@
 POINTS = LEAVES * CAPACITY
 LEAF_LANES = LEAVES * RANK_LEAF
 MID_LANES = GROUPS * RANK
-PARTS = 8
+PARTS = 4
 PART = SLOTS * CAPACITY // PARTS
 BLOCK = SLOTS // PARTS
 WIDE = POINTS + LEAF_LANES + MID_LANES
 LANES = 128
 VMEM_LIMIT = 60 * 1024 * 1024
+UP_LIMIT = 60 * 1024 * 1024
+SIDE_LIMIT = 51500 * 1024
+DOWN_LIMIT = 54400 * 1024
 MESSAGES = 16
 LEAF_AT = LEAVES // 2
 MID_AT = LEAF_AT + LEAVES // 4
 FIELDS = MID_AT + GROUPS // 2
+
+
+HBM = pl.BlockSpec(memory_space=pltpu.HBM)
 
 
 def dot_nt(left, right):
@@ -68,17 +74,22 @@
     basis_hbm,
     leaf_hbm,
     mid_hbm,
+    top_hbm,
     packed_hbm,
     message_hbm,
+    parents_hbm,
     charges,
     basis,
     leaf_transfer,
     mid_transfer,
     coefficients,
     message,
+    parents,
     sem,
     out_sem,
+    parent_sem,
 ):
+    device = lax.axis_index("clusters")
     copies = [
         pltpu.make_async_copy(a, b, sem.at[i])
         for i, (a, b) in enumerate(
@@ -92,6 +103,17 @@
     ]
     for copy in copies:
         copy.start()
+    parent_copies = []
+    for level in range(LEVELS):
+        start = BOXES - (BOXES >> level)
+        parent_copies.append(
+            pltpu.make_async_copy(
+                top_hbm.at[start + (device >> (level + 1))],
+                parents.at[level],
+                parent_sem.at[level],
+            )
+        )
+        parent_copies[level].start()
     lane = lane_index((VECTORS, LANES))
     wide_lane = lane_index((VECTORS, 4 * CAPACITY)) // CAPACITY
     copies[0].wait()
@@ -134,6 +156,10 @@
         coefficients, packed_hbm.at[:, pl.ds(POINTS, LEAF_LANES + MID_LANES)], out_sem.at[1]
     )
     coefficients_out.start()
+    for copy in parent_copies:
+        copy.wait()
+    parents_out = pltpu.make_async_copy(parents, parents_hbm, parent_sem.at[LEVELS])
+    parents_out.start()
     copies[3].wait()
     box = dot_nt(jnp.concatenate(mid, axis=1), mid_transfer[0])
     box = jnp.concatenate([box[:4], box[4:]], axis=1)
@@ -149,6 +175,7 @@
         copy.start()
     charges_out.wait()
     coefficients_out.wait()
+    parents_out.wait()
     for copy in messages_out:
         copy.wait()
 
@@ -162,10 +189,10 @@
     own_hbm,
     pair_hbm,
     other_hbm,
-    far_hbm,
-    mid_far_hbm,
+    far,
+    mid_coupling,
     top_coupling_hbm,
-    top_transfer_hbm,
+    parents_hbm,
     box_coupling_hbm,
     near_hbm,
     field_hbm,
@@ -177,8 +204,6 @@
     own,
     pair,
     other,
-    far,
-    mid_coupling,
     top_coupling,
     parents,
     box_coupling,
@@ -230,26 +255,14 @@
                 (pair_hbm, pair),
                 (other_hbm, other),
                 (box_coupling_hbm, box_coupling),
-                (far_hbm, far),
-                (mid_far_hbm, mid_coupling),
                 (top_coupling_hbm, top_coupling),
             )
         )
     ]
-    parent_copies = []
-    for level in range(LEVELS):
-        start = BOXES - (BOXES >> level)
-        parent_copies.append(
-            pltpu.make_async_copy(
-                top_transfer_hbm.at[start + (device >> (level + 1))],
-                parents.at[level],
-                parent_sem.at[level],
-            )
-        )
+    parent_copies = [pltpu.make_async_copy(parents_hbm, parents, parent_sem)]
     for copy in copies[:8]:
         copy.start()
     near_copy(0).start()
-    near_copy(1).start()
     for copy in parent_copies:
         copy.start()
     copies[8].start()
@@ -278,12 +291,11 @@
     ]
     for copy in index_copies:
         copy.start()
-    blocks = jnp.clip((live + BLOCK - 1) // BLOCK, 2, PARTS)
-    for k in (2, 3):
-
-        @pl.when(k < blocks)
-        def _(k=k):
-            near_copy(k).start()
+    blocks = jnp.clip((live + BLOCK - 1) // BLOCK, 1, PARTS)
+
+    @pl.when(blocks > 1)
+    def _():
+        near_copy(1).start()
 
     lane = lane_index((VECTORS, LANES))
     zero = jnp.zeros((VECTORS, LANES), F32)
@@ -323,25 +335,22 @@
     zeros_half = jnp.zeros((2 * VECTORS, LANES), BF16)
 
     def near_step(k, carry):
-        @pl.when(k + 4 < blocks)
+        @pl.when(k + 2 < blocks)
         def _():
-            near_copy(k + 4).start()
+            near_copy(k + 2).start()
 
         @pl.when(k == 0)
         def _():
             copies[9].start()
-            copies[10].start()
-
-        @pl.when(k == 1)
-        def _():
-            copies[11].start()
 
         near_copy(k).wait()
+        sources = [near_from.at[2 * k + i] for i in range(2)]
+        targets = [near_to.at[2 * k + i] for i in range(2)]
         for i in range(BLOCK // 16):
             rows, weights = [], []
             for g in range(4):
                 first = 16 * i + 4 * g
-                at = [rows_of(near_from[k, first + j]) for j in range(4)]
+                at = [rows_of(sources[first // LANES][first % LANES + j]) for j in range(4)]
                 top = jnp.concatenate([x_low[at[0], :], x_high[at[1], :]], axis=0)
                 bottom = jnp.concatenate([x_low[at[2], :], x_high[at[3], :]], axis=0)
                 rows.append(jnp.concatenate([top.astype(BF16), zeros_half], axis=1))
@@ -349,8 +358,9 @@
                 weights.append(near[k, :, first * CAPACITY : (first + 4) * CAPACITY])
             result = dot_nt(jnp.concatenate(rows, axis=0), jnp.concatenate(weights, axis=0))
             for g in range(4):
+                first = 16 * i + 4 * g
                 for j in range(4):
-                    to = rows_of(near_to[k, 16 * i + 4 * g + j])
+                    to = rows_of(targets[first // LANES][first % LANES + j])
                     at = 32 * g + 8 * j
                     accumulators[g][to, :] += result[
                         at : at + 8, (g // 2) * LANES : (g // 2 + 1) * LANES
@@ -380,7 +390,6 @@
         product = dot_nt(product.astype(BF16), own_half.astype(BF16))
         products.append(product.astype(BF16))
 
-    copies[9].wait()
     for group in range(LEAVES // 8):
         rows = []
         for i in range(8):
@@ -409,7 +418,6 @@
                     for j in range(4)
                 ],
             )
-    copies[10].wait()
     rows = []
     for c in range(GROUPS):
         rows.append(
@@ -437,16 +445,28 @@
     field_out = pltpu.make_async_copy(field, field_hbm, out_sem.at[0])
     field_out.start()
 
-    copies[11].wait()
-    tops = top_coupling.shape[2]
-    level = lax.broadcasted_iota(jnp.int32, (VECTORS, tops), 0) + 1
+    copies[9].wait()
+    level = lax.broadcasted_iota(jnp.int32, (VECTORS, LANES), 0) + 1
     column = BOXES - lax.shift_right_logical(jnp.full_like(level, BOXES), level - 1)
     column = column + lax.shift_right_logical(jnp.full_like(level, 1) * device, level)
-    wanted = (lane_index((VECTORS, tops)) == column).astype(F32).astype(BF16)
-    for r in range(RANK):
-        result = dot_nt(wanted, top_coupling[r])
-        chosen_low[r * VECTORS : (r + 1) * VECTORS, :] = result[:, :LANES]
-        chosen_high[r * VECTORS : (r + 1) * VECTORS, 0:RANK] = result[:, LANES:]
+    wanted = (lane_index(level.shape) == column).astype(F32)
+    nothing = jnp.zeros_like(wanted)
+    wanted = jnp.concatenate(
+        [
+            jnp.concatenate([wanted, nothing], axis=1),
+            jnp.concatenate([nothing, wanted], axis=1),
+        ],
+        axis=0,
+    ).astype(BF16)
+    missing = jnp.zeros((3 * RANK, 4), BF16)
+    for r in range(0, RANK, 2):
+        columns = [
+            jnp.concatenate([top_coupling[r + i], missing], axis=1) for i in range(2)
+        ]
+        result = dot_nt(wanted, jnp.concatenate(columns, axis=1))
+        rows = slice(r * VECTORS, (r + 2) * VECTORS)
+        chosen_low[rows, :] = result[:, :LANES]
+        chosen_high[rows, 0:RANK] = result[:, LANES:]
     copies[8].wait()
     coupling[0] = box_coupling[0]
     for k in range(LEVELS):
@@ -460,20 +480,17 @@
 
 
 def down_kernel(
-    every_hbm,
+    every,
     top_hbm,
-    coupling_hbm,
+    coupling,
     mid_hbm,
     leaf_hbm,
-    field_hbm,
+    field,
     basis_hbm,
     out,
-    every,
     top_transfer,
-    coupling,
     mid_transfer,
     leaf_transfer,
-    field,
     basis,
     sem,
     pairs0,
@@ -489,13 +506,10 @@
         pltpu.make_async_copy(source, target, sem.at[i])
         for i, (source, target) in enumerate(
             (
-                (every_hbm, every),
                 (top_hbm.at[half], top_transfer.at[half]),
                 (top_hbm.at[rest], top_transfer.at[rest]),
-                (coupling_hbm, coupling),
                 (mid_hbm, mid_transfer),
                 (leaf_hbm, leaf_transfer),
-                (field_hbm, field),
                 (basis_hbm, basis),
             )
         )
@@ -511,14 +525,13 @@
     for level in range(LEVELS + 1):
         pairs[level][0] = zero
         pairs[level][(BOXES >> (level + 1)) + 1] = zero
-    copies[0].wait()
     kept = (lane < RANK) == (lax.broadcasted_iota(jnp.int32, (VECTORS, LANES), 0) < 4)
     for p in range(BOXES // 2):
         tile = every[p].astype(F32)
         pairs0[p + 1] = jnp.where(kept, tile, pltpu.roll(pltpu.roll(tile, RANK, 1), 4, 0))
     for level in range(LEVELS):
         if level < 2:
-            copies[1 + level].wait()
+            copies[level].wait()
         start = BOXES - (BOXES >> level)
         count = BOXES >> (level + 1)
         for g in range(0, count, 8):
@@ -537,7 +550,6 @@
                 pairs[level + 1][1 + g // 2 + i] = pick_two(
                     lane, result[16 * i : 16 * i + 8, span], result[16 * i + 8 : 16 * i + 16, span]
                 )
-    copies[3].wait()
     down = jnp.zeros((VECTORS, RANK), F32)
     for level in range(LEVELS + 1):
         cluster = device >> level
@@ -548,10 +560,9 @@
         stacked = jnp.concatenate([pick_two(lane, before, middle), after[:, :64]], axis=1)
         down = down + dot_nt(stacked.astype(BF16), coupling[level])
 
-    copies[4].wait()
+    copies[2].wait()
     mid_push = dot_nn(down.astype(BF16), mid_transfer[0])
-    copies[5].wait()
-    copies[6].wait()
+    copies[3].wait()
     rows = []
     for c in range(GROUPS):
         h = c // 2
@@ -564,7 +575,7 @@
         jnp.concatenate(rows, axis=0).astype(BF16),
         leaf_transfer[...].reshape(GROUPS * RANK, CHILDREN * RANK_LEAF),
     )
-    copies[7].wait()
+    copies[4].wait()
     lane_group = lane // RANK_LEAF
     for first in range(0, LEAVES // 4, 8):
         rows, weights = [], []
@@ -590,35 +601,18 @@
                 )
 
 
-def body(
-    charges,
-    leaf_basis,
-    leaf_transfer,
-    mid_transfer,
-    far_source,
-    far_coupling,
-    mid_source,
-    mid_coupling,
-    box_coupling,
-    top_transfer,
-    top_coupling,
-    near_target,
-    near_source,
-    near_count,
-    near_blocks,
-):
-    pair = [(i, i ^ 1) for i in range(BOXES)]
-    other = [(i, min(max(((i + 1) ^ 1) - 1, 0), BOXES - 1)) for i in range(BOXES)]
-    vmem = pl.BlockSpec(memory_space=pltpu.VMEM)
-    hbm = pl.BlockSpec(memory_space=pltpu.HBM)
-    shape = jax.ShapeDtypeStruct
-    scratch = pltpu.VMEM
+def up_call(*operands):
+    hbm, shape, scratch = HBM, jax.ShapeDtypeStruct, pltpu.VMEM
     dma = pltpu.SemaphoreType.DMA
-    packed, message = pl.pallas_call(
+    return pl.pallas_call(
         up_kernel,
-        out_shape=(shape((VECTORS, WIDE), BF16), shape((BOXES // 2, VECTORS, LANES), BF16)),
-        in_specs=[hbm] * 4,
-        out_specs=(hbm, hbm),
+        out_shape=(
+            shape((VECTORS, WIDE), BF16),
+            shape((BOXES // 2, VECTORS, LANES), BF16),
+            shape((LEVELS, RANK, 2 * RANK), BF16),
+        ),
+        in_specs=[hbm] * 5,
+        out_specs=(hbm, hbm, hbm),
         scratch_shapes=[
             scratch((VECTORS, POINTS), BF16),
             scratch((RANK_LEAF, POINTS), BF16),
@@ -626,16 +620,35 @@
             scratch((1, RANK, GROUPS * RANK), BF16),
             scratch((VECTORS, LEAF_LANES + MID_LANES), BF16),
             scratch((MESSAGES, VECTORS, LANES), BF16),
+            scratch((LEVELS, RANK, 2 * RANK), BF16),
             dma((4,)),
             dma((2 + BOXES // 2 // MESSAGES,)),
+            dma((LEVELS + 1,)),
         ],
         cost_estimate=pl.CostEstimate(flops=10**9, bytes_accessed=10**6, transcendentals=0),
-        compiler_params=pltpu.CompilerParams(vmem_limit_bytes=VMEM_LIMIT),
+        compiler_params=pltpu.CompilerParams(vmem_limit_bytes=UP_LIMIT),
         name="upward",
-    )(charges, leaf_basis, leaf_transfer, mid_transfer)
-    packed_other = lax.ppermute(packed, "clusters", other)
-    packed_pair = lax.ppermute(packed, "clusters", pair)
-    every = lax.all_to_all(message.reshape(BOXES, VECTORS // 2, LANES), "clusters", 0, 0)
+    )(*operands)
+
+
+def side_call(
+    near_source,
+    near_target,
+    near_count,
+    far_source,
+    mid_source,
+    packed,
+    packed_pair,
+    packed_other,
+    far_coupling,
+    mid_coupling,
+    top_coupling,
+    parents,
+    box_coupling,
+    near_blocks,
+):
+    hbm, shape, scratch = HBM, jax.ShapeDtypeStruct, pltpu.VMEM
+    dma = pltpu.SemaphoreType.DMA
     table = scratch((3 * LEAVES * VECTORS, LANES), F32)
     accumulator = scratch(((LEAVES + 1) * VECTORS, LANES), F32)
     indices = [
@@ -645,21 +658,19 @@
         (GROUPS, MID_FAR),
     ]
     wide = scratch((VECTORS, WIDE), BF16)
-    field, coupling = pl.pallas_call(
+    return pl.pallas_call(
         side_kernel,
         out_shape=(
             shape((FIELDS, VECTORS, LANES), F32),
             shape((LEVELS + 1, RANK, 3 * RANK), BF16),
         ),
-        in_specs=[hbm] * 14,
+        in_specs=[hbm] * 8 + [pl.BlockSpec(memory_space=pltpu.VMEM)] * 2 + [hbm] * 4,
         out_specs=(hbm, hbm),
         scratch_shapes=[scratch(i, jnp.int32) for i in indices]
         + [
             wide,
             wide,
             wide,
-            scratch((LEAVES, RANK_LEAF, FAR * RANK_LEAF), BF16),
-            scratch((GROUPS, RANK, MID_FAR * RANK), BF16),
             scratch((RANK, 3 * RANK, BOXES - 4), BF16),
             scratch((LEVELS, RANK, 2 * RANK), BF16),
             scratch((1, RANK, 3 * RANK), BF16),
@@ -680,9 +691,9 @@
         + [scratch(i, jnp.int32) for i in indices]
         + [pltpu.SMEM((1, 1), jnp.int32)]
         + [pltpu.SMEM(i, jnp.int32) for i in indices]
-        + [dma((PARTS,)), dma((12,)), dma((LEVELS,)), dma((4,)), dma((2,))],
+        + [dma((PARTS,)), dma((10,)), dma, dma((4,)), dma((2,))],
         cost_estimate=pl.CostEstimate(flops=2 * 10**9, bytes_accessed=10**7, transcendentals=0),
-        compiler_params=pltpu.CompilerParams(vmem_limit_bytes=VMEM_LIMIT),
+        compiler_params=pltpu.CompilerParams(vmem_limit_bytes=SIDE_LIMIT),
         name="side",
     )(
         near_source.reshape(VECTORS, LANES),
@@ -696,33 +707,88 @@
         far_coupling,
         mid_coupling,
         jnp.transpose(top_coupling, (1, 2, 0)),
-        top_transfer,
+        parents,
         box_coupling,
         near_blocks,
     )
+
+
+def down_call(*operands):
+    hbm, shape, scratch = HBM, jax.ShapeDtypeStruct, pltpu.VMEM
+    dma = pltpu.SemaphoreType.DMA
+    vmem = pl.BlockSpec(memory_space=pltpu.VMEM)
     return pl.pallas_call(
         down_kernel,
         out_shape=shape((VECTORS, POINTS), BF16),
-        in_specs=[hbm] * 7,
-        out_specs=vmem,
+        in_specs=[vmem, hbm, vmem, hbm, hbm, vmem, hbm],
+        out_specs=pl.BlockSpec(memory_space=pltpu.VMEM),
         scratch_shapes=[
-            scratch((BOXES // 2, VECTORS, LANES), BF16),
             scratch((BOXES - 4, RANK, 2 * RANK), BF16),
-            scratch((LEVELS + 1, RANK, 3 * RANK), BF16),
             scratch((1, RANK, GROUPS * RANK), BF16),
             scratch((GROUPS, RANK, CHILDREN * RANK_LEAF), BF16),
-            scratch((FIELDS, VECTORS, LANES), F32),
             scratch((RANK_LEAF, POINTS), BF16),
-            dma((8,)),
+            dma((5,)),
         ]
         + [
             scratch(((BOXES >> (level + 1)) + 2, VECTORS, LANES), F32)
             for level in range(LEVELS + 1)
         ],
         cost_estimate=pl.CostEstimate(flops=10**9, bytes_accessed=10**6, transcendentals=0),
-        compiler_params=pltpu.CompilerParams(vmem_limit_bytes=VMEM_LIMIT),
+        compiler_params=pltpu.CompilerParams(vmem_limit_bytes=DOWN_LIMIT),
         name="down",
-    )(every.reshape(BOXES // 2, VECTORS, LANES), top_transfer, coupling, mid_transfer, leaf_transfer, field, leaf_basis)
+    )(*operands)
+
+
+def body(
+    charges,
+    leaf_basis,
+    leaf_transfer,
+    mid_transfer,
+    far_source,
+    far_coupling,
+    mid_source,
+    mid_coupling,
+    box_coupling,
+    top_transfer,
+    top_coupling,
+    near_target,
+    near_source,
+    near_count,
+    near_blocks,
+):
+    pair = [(i, i ^ 1) for i in range(BOXES)]
+    other = [(i, min(max(((i + 1) ^ 1) - 1, 0), BOXES - 1)) for i in range(BOXES)]
+    packed, message, parents = up_call(
+        charges, leaf_basis, leaf_transfer, mid_transfer, top_transfer
+    )
+    packed_other = lax.ppermute(packed, "clusters", other)
+    packed_pair = lax.ppermute(packed, "clusters", pair)
+    every = lax.all_to_all(message.reshape(BOXES, VECTORS // 2, LANES), "clusters", 0, 0)
+    field, coupling = side_call(
+        near_source,
+        near_target,
+        near_count,
+        far_source,
+        mid_source,
+        packed,
+        packed_pair,
+        packed_other,
+        far_coupling,
+        mid_coupling,
+        top_coupling,
+        parents,
+        box_coupling,
+        near_blocks,
+    )
+    return down_call(
+        every.reshape(BOXES // 2, VECTORS, LANES),
+        top_transfer,
+        coupling,
+        mid_transfer,
+        leaf_transfer,
+        field,
+        leaf_basis,
+    )
 
 
 def solution(mesh):

time: 33.2 us -> 32.1 us (0.967)
  Pallas kernels: 17.7 us -> 15.9 us
  local copies, waits for them, and re-layouts: 1.31 us -> 1.81 us
    pallas_call x3, Pallas kernels: 17.7 us -> 15.9 us  [the longest x1 9.42 us: side_call(): pl.pallas_call(side_kernel, out_shape=(shape((FIELDS, VECTORS, LANES), F3...]
    unnamed x6 -> x20, local copies, waits for them, and re-layouts: 1.31 us -> 1.81 us
  transfers between devices with their start and end apart: 3 -> 3, of which waited for: 0 -> 0; matrix products, arithmetic and copies ran while one was open for 0% -> 0% of each run, Pallas kernels for 34% -> 30%
where the time goes in v3:
time: 32.1 us; the launch traced here: 31.8 us
  Pallas kernels  15.9 us (50%)
  starting transfers between devices  13.3 us (41%)
  local copies, waits for them, and re-layouts  1.81 us (6%)
  between operations  0.81 us (3%)
    all_to_all x1, starting transfers between devices, body(): lax.all_to_all(message.reshape(BOXES, VECTORS // 2, LANES), 'clusters', 0...  10.3 us
    pallas_call x1, Pallas kernels, side_call(): pl.pallas_call(side_kernel, out_shape=(shape((FIELDS, VECTORS, LANES), F3...  9.42 us
    pallas_call x1, Pallas kernels, down_call(): pl.pallas_call(down_kernel, out_shape=shape((VECTORS, POINTS), BF16), in_...  3.79 us
    pallas_call x1, Pallas kernels, up_call(): pl.pallas_call(up_kernel, out_shape=(shape((VECTORS, WIDE), BF16), shape(...  2.7 us
    unnamed x20, local copies, waits for them, and re-layouts  1.81 us
    ppermute x1, starting transfers between devices, body(): packed_other = lax.ppermute(packed, 'clusters', other)  1.55 us
    ppermute x1, starting transfers between devices, body(): packed_pair = lax.ppermute(packed, 'clusters', pair)  1.38 us
  transfers between devices with their start and end apart: 3, of which 0 were waited for; matrix products, arithmetic and copies ran while one was open for 0% of the time, Pallas kernels for 30%

profile of v3, /device:TPU:127, one launch (start us, length us, event | category | flops | bytes accessed | tf_op | source)
XLA Modules:
  0.0 31.8 jit_solution(18124851879828688253)
XLA Ops:
  0.0 0.0 copy-start.6
  0.0 0.0 copy-start.7
  0.0 0.0 copy-start.4
  0.0 0.0 copy-start.1
  0.0 0.0 copy-start.8
  0.0 0.0 copy-start
  0.0 0.0 copy-start.5
  0.0 2.7 %upward.1 = (bf16[8,6656]{1,0:T(8,128)(2,1)}, bf16[64,8,128]{2,1,0:T(8,128)(2,1)}, bf16[5,64,128]{2,1,0:T(8,128)(2,1)}) custom-call(bf16[8,4096]{1,0:T(8,128)(2,1)} %charges_hbm.1, bf16[32,4096]{1,0:T(8,128)(2,1)} %basis_hbm.3, bf16[8,64,256]{2,1,0:T(8,128)(2,1)} %leaf_hbm.3, bf16[1,64,512]{2,1,0:T(8,128)(2,1)} %mid_hbm.3, bf16[124,64,128]{2,1,0:T(8,128)(2,1)} %top_hbm.3), custom_call_target="tpu_custom_call" | custom-call | flops 1000000000 | bytes 1000000 | tf_op jit(solution)/shard_map/upward/pallas_call | solution.py:607
  2.8 1.6 %collective-permute-start.1 = (bf16[8,6656]{1,0:T(8,128)(2,1)}, bf16[8,6656]{1,0:T(8,128)(2,1)S(1)}, u32[]{:S(2)}, u32[]{:S(2)}) collective-permute-start(bf16[8,6656]{1,0:T(8,128)(2,1)} %get-tuple-element.11.own_hbm), channel_id=1, source_target_pairs={{0,0},{1,2},{2,1},{3,4},{4,3},{5,6},{6,5},{7,8},{8,7},{9,10},{10,9... | collective-permute-start | bytes 319496 | tf_op jit(solution)/shard_map/ppermute | solution.py:764
  4.3 1.4 %collective-permute-start = (bf16[8,6656]{1,0:T(8,128)(2,1)}, bf16[8,6656]{1,0:T(8,128)(2,1)S(1)}, u32[]{:S(2)}, u32[]{:S(2)}) collective-permute-start(bf16[8,6656]{1,0:T(8,128)(2,1)} %get-tuple-element.11.own_hbm), channel_id=1, source_target_pairs={{0,1},{1,0},{2,3},{3,2},{4,5},{5,4},{6,7},{7,6},{8,9},{9,8},{10,11... | collective-permute-start | bytes 319496 | tf_op jit(solution)/shard_map/ppermute | solution.py:765
  5.7 10.3 %all-to-all-start = ((bf16[128,4,128]{2,1,0:T(4,128)(2,1)}), bf16[128,4,128]{2,1,0:T(4,128)(2,1)S(1)}, u32[]{:S(2)}, u32[]{:S(2)}) async-start(bf16[128,4,128]{2,1,0:T(4,128)(2,1)} %bitcast.13), calls=%async_computation | async-start | bytes 262144 | tf_op jit(solution)/shard_map/all_to_all | solution.py:766
  16.7 0.0 collective-permute-done.1.other_hbm
  16.7 0.0 collective-permute-done.pair_hbm
  16.7 0.0 copy-done.6
  16.7 0.0 copy-done.7
  16.7 0.0 copy-done.4
  16.7 0.0 copy-done.1
  16.7 0.0 copy-done.8
  16.8 0.0 copy-done
  16.8 0.0 copy-done.5
  16.8 0.0 copy-start.2
  16.8 0.9 %copy-done.2 = bf16[8,6656]{1,0:T(8,128)(2,1)S(1)} copy-done((bf16[8,6656]{1,0:T(8,128)(2,1)S(1)}, bf16[8,6656]{1,0:T(8,128)(2,1)}, u32[]{:S(2)}) %copy-start.2) | copy-done | bytes 106520
  17.7 0.0 copy-start.3
  17.7 0.9 %copy-done.3 = bf16[5,64,128]{2,1,0:T(8,128)(2,1)S(1)} copy-done((bf16[5,64,128]{2,1,0:T(8,128)(2,1)S(1)}, bf16[5,64,128]{2,1,0:T(8,128)(2,1)}, u32[]{:S(2)}) %copy-start.3) | copy-done | bytes 81944
  18.6 0.0 copy-start.9
  18.6 9.4 %side.1 = (f32[52,8,128]{2,1,0:T(8,128)S(1)}, bf16[6,64,192]{2,1,0:T(8,128)(2,1)S(1)}) custom-call(s32[8,128]{1,0:T(8,128)S(1)} %bitcast.10, s32[8,128]{1,0:T(8,128)S(1)} %bitcast.11, s32[1,1]{1,0:T(1,128)} %bitcast.7.near_count_hbm, s32[16,64]{1,0:T(8,128)S(1)} %bitcast.9, s32[8,8]{1,0:T(8,128)S(1)} %copy-done.8, bf16[8,6656]{1,0:T(8,128)(2,1)S(1)} %copy-done.2, ...), custom_call_target="tpu_custom_call" | custom-call | flops 2000000000 | bytes 10000000 | tf_op jit(solution)/shard_map/side/pallas_call | solution.py:661
  28.0 0.0 all-to-all-done
  28.0 0.0 copy-done.9
  28.0 3.8 %down.1 = bf16[8,4096]{1,0:T(8,128)(2,1)} custom-call(bf16[64,8,128]{2,1,0:T(8,128)(2,1)S(1)} %bitcast.8, bf16[124,64,128]{2,1,0:T(8,128)(2,1)} %top_hbm.3, bf16[6,64,192]{2,1,0:T(8,128)(2,1)S(1)} %get-tuple-element.13.coupling, bf16[1,64,512]{2,1,0:T(8,128)(2,1)S(1)} %copy-done.9, bf16[8,64,256]{2,1,0:T(8,128)(2,1)} %leaf_hbm.3, ...), custom_call_target="tpu_custom_call" | custom-call | flops 1000000000 | bytes 1000000 | tf_op jit(solution)/shard_map/down/pallas_call | solution.py:720
Async XLA Ops:
  0.0 16.7 %copy-start.6 = (s32[1024]{0:T(1024)S(1)}, s32[1024]{0:T(1024)}, u32[]{:S(2)}) copy-start(s32[1024]{0:T(1024)} %param.27) | copy-start | bytes 12292
  0.0 16.7 %copy-start.7 = (s32[1024]{0:T(1024)S(1)}, s32[1024]{0:T(1024)}, u32[]{:S(2)}) copy-start(s32[1024]{0:T(1024)} %param.26) | copy-start | bytes 12292
  0.0 16.7 %copy-start.4 = (bf16[1,64,192]{2,1,0:T(8,128)(2,1)S(1)}, bf16[1,64,192]{2,1,0:T(8,128)(2,1)}, u32[]{:S(2)}) copy-start(bf16[1,64,192]{2,1,0:T(8,128)(2,1)} %box_coupling_hbm.1) | copy-start | bytes 73732
  0.0 16.7 %copy-start.1 = (bf16[8,64,512]{2,1,0:T(8,128)(2,1)S(1)}, bf16[8,64,512]{2,1,0:T(8,128)(2,1)}, u32[]{:S(2)}) copy-start(bf16[8,64,512]{2,1,0:T(8,128)(2,1)} %mid_coupling.1) | copy-start | bytes 1572868
  0.0 16.7 %copy-start.8 = (s32[8,8]{1,0:T(8,128)S(1)}, s32[8,8]{1,0:T(8,128)}, u32[]{:S(2)}) copy-start(s32[8,8]{1,0:T(8,128)} %mid_source_hbm.1) | copy-start | bytes 772
  0.0 16.7 %copy-start = (bf16[64,32,512]{2,1,0:T(8,128)(2,1)S(1)}, bf16[64,32,512]{2,1,0:T(8,128)(2,1)}, u32[]{:S(2)}) copy-start(bf16[64,32,512]{2,1,0:T(8,128)(2,1)} %far.1) | copy-start | bytes 6291460
  0.0 16.7 %copy-start.5 = (s32[64,16]{0,1:T(8,128)S(1)}, s32[64,16]{0,1:T(8,128)}, u32[]{:S(2)}) copy-start(s32[64,16]{0,1:T(8,128)} %param.19) | copy-start | bytes 12292
  2.8 13.9 %collective-permute-start.1 = (bf16[8,6656]{1,0:T(8,128)(2,1)}, bf16[8,6656]{1,0:T(8,128)(2,1)S(1)}, u32[]{:S(2)}, u32[]{:S(2)}) collective-permute-start(bf16[8,6656]{1,0:T(8,128)(2,1)} %get-tuple-element.11.own_hbm), channel_id=1, source_target_pairs={{0,0},{1,2},{2,1},{3,4},{4,3},{5,6},{6,5},{7,8},{8,7},{9,10},{10,9... | collective-permute-start | bytes 319496 | tf_op jit(solution)/shard_map/ppermute | solution.py:764
  4.3 12.4 %collective-permute-start = (bf16[8,6656]{1,0:T(8,128)(2,1)}, bf16[8,6656]{1,0:T(8,128)(2,1)S(1)}, u32[]{:S(2)}, u32[]{:S(2)}) collective-permute-start(bf16[8,6656]{1,0:T(8,128)(2,1)} %get-tuple-element.11.own_hbm), channel_id=1, source_target_pairs={{0,1},{1,0},{2,3},{3,2},{4,5},{5,4},{6,7},{7,6},{8,9},{9,8},{10,11... | collective-permute-start | bytes 319496 | tf_op jit(solution)/shard_map/ppermute | solution.py:765
  5.7 22.3 %all-to-all-start = ((bf16[128,4,128]{2,1,0:T(4,128)(2,1)}), bf16[128,4,128]{2,1,0:T(4,128)(2,1)S(1)}, u32[]{:S(2)}, u32[]{:S(2)}) async-start(bf16[128,4,128]{2,1,0:T(4,128)(2,1)} %bitcast.13), calls=%async_computation | async-start | bytes 262144 | tf_op jit(solution)/shard_map/all_to_all | solution.py:766
  16.8 0.9 %copy-start.2 = (bf16[8,6656]{1,0:T(8,128)(2,1)S(1)}, bf16[8,6656]{1,0:T(8,128)(2,1)}, u32[]{:S(2)}) copy-start(bf16[8,6656]{1,0:T(8,128)(2,1)} %get-tuple-element.11.own_hbm) | copy-start | bytes 319492
  17.7 0.9 %copy-start.3 = (bf16[5,64,128]{2,1,0:T(8,128)(2,1)S(1)}, bf16[5,64,128]{2,1,0:T(8,128)(2,1)}, u32[]{:S(2)}) copy-start(bf16[5,64,128]{2,1,0:T(8,128)(2,1)} %get-tuple-element.12.parents_hbm) | copy-start | bytes 245764
  18.6 9.4 %copy-start.9 = (bf16[1,64,512]{2,1,0:T(8,128)(2,1)S(1)}, bf16[1,64,512]{2,1,0:T(8,128)(2,1)}, u32[]{:S(2)}) copy-start(bf16[1,64,512]{2,1,0:T(8,128)(2,1)} %mid_hbm.3) | copy-start | bytes 196612

commit v4 on v3

--- a/solution.py
+++ b/solution.py
@@ -29,6 +29,7 @@
 WIDE = POINTS + LEAF_LANES + MID_LANES
 LANES = 128
 VMEM_LIMIT = 60 * 1024 * 1024
+LOCAL = WIDE + LEVELS * RANK * LANES // VECTORS
 UP_LIMIT = 60 * 1024 * 1024
 SIDE_LIMIT = 51500 * 1024
 DOWN_LIMIT = 54400 * 1024
@@ -77,7 +78,7 @@
     top_hbm,
     packed_hbm,
     message_hbm,
-    parents_hbm,
+    local_hbm,
     charges,
     basis,
     leaf_transfer,
@@ -85,6 +86,7 @@
     coefficients,
     message,
     parents,
+    local,
     sem,
     out_sem,
     parent_sem,
@@ -158,8 +160,14 @@
     coefficients_out.start()
     for copy in parent_copies:
         copy.wait()
-    parents_out = pltpu.make_async_copy(parents, parents_hbm, parent_sem.at[LEVELS])
-    parents_out.start()
+    local[:, pl.ds(0, POINTS)] = charges[...]
+    local[:, pl.ds(POINTS, LEAF_LANES + MID_LANES)] = coefficients[...]
+    for level in range(LEVELS):
+        for i in range(RANK // VECTORS):
+            at = WIDE + (level * (RANK // VECTORS) + i) * LANES
+            local[:, pl.ds(at, LANES)] = parents[level, i * VECTORS : (i + 1) * VECTORS, :]
+    local_out = pltpu.make_async_copy(local, local_hbm, parent_sem.at[LEVELS])
+    local_out.start()
     copies[3].wait()
     box = dot_nt(jnp.concatenate(mid, axis=1), mid_transfer[0])
     box = jnp.concatenate([box[:4], box[4:]], axis=1)
@@ -175,7 +183,7 @@
         copy.start()
     charges_out.wait()
     coefficients_out.wait()
-    parents_out.wait()
+    local_out.wait()
     for copy in messages_out:
         copy.wait()
 
@@ -192,7 +200,6 @@
     far,
     mid_coupling,
     top_coupling_hbm,
-    parents_hbm,
     box_coupling_hbm,
     near_hbm,
     field_hbm,
@@ -205,7 +212,6 @@
     pair,
     other,
     top_coupling,
-    parents,
     box_coupling,
     near,
     field,
@@ -231,7 +237,6 @@
     mid_from,
     near_sem,
     sem,
-    parent_sem,
     index_sem,
     out_sem,
 ):
@@ -259,12 +264,10 @@
             )
         )
     ]
-    parent_copies = [pltpu.make_async_copy(parents_hbm, parents, parent_sem)]
     for copy in copies[:8]:
         copy.start()
+    copies[9].start()
     near_copy(0).start()
-    for copy in parent_copies:
-        copy.start()
     copies[8].start()
 
     for copy in copies[:5]:
@@ -292,10 +295,6 @@
     for copy in index_copies:
         copy.start()
     blocks = jnp.clip((live + BLOCK - 1) // BLOCK, 1, PARTS)
-
-    @pl.when(blocks > 1)
-    def _():
-        near_copy(1).start()
 
     lane = lane_index((VECTORS, LANES))
     zero = jnp.zeros((VECTORS, LANES), F32)
@@ -332,58 +331,21 @@
     for copy in index_copies:
         copy.wait()
 
-    zeros_half = jnp.zeros((2 * VECTORS, LANES), BF16)
-
-    def near_step(k, carry):
-        @pl.when(k + 2 < blocks)
-        def _():
-            near_copy(k + 2).start()
-
-        @pl.when(k == 0)
-        def _():
-            copies[9].start()
-
-        near_copy(k).wait()
-        sources = [near_from.at[2 * k + i] for i in range(2)]
-        targets = [near_to.at[2 * k + i] for i in range(2)]
-        for i in range(BLOCK // 16):
-            rows, weights = [], []
-            for g in range(4):
-                first = 16 * i + 4 * g
-                at = [rows_of(sources[first // LANES][first % LANES + j]) for j in range(4)]
-                top = jnp.concatenate([x_low[at[0], :], x_high[at[1], :]], axis=0)
-                bottom = jnp.concatenate([x_low[at[2], :], x_high[at[3], :]], axis=0)
-                rows.append(jnp.concatenate([top.astype(BF16), zeros_half], axis=1))
-                rows.append(jnp.concatenate([zeros_half, bottom.astype(BF16)], axis=1))
-                weights.append(near[k, :, first * CAPACITY : (first + 4) * CAPACITY])
-            result = dot_nt(jnp.concatenate(rows, axis=0), jnp.concatenate(weights, axis=0))
-            for g in range(4):
-                first = 16 * i + 4 * g
-                for j in range(4):
-                    to = rows_of(targets[first // LANES][first % LANES + j])
-                    at = 32 * g + 8 * j
-                    accumulators[g][to, :] += result[
-                        at : at + 8, (g // 2) * LANES : (g // 2 + 1) * LANES
-                    ]
-        return carry
-
-    lax.fori_loop(0, blocks, near_step, 0)
-    for h in range(LEAVES // 2):
-        low = rows_of(2 * h * VECTORS)
-        high = rows_of((2 * h + 1) * VECTORS)
-        placed = pick_two(lane, acc0[low, :] + acc2[low, :], acc1[high, :] + acc3[high, :])
-        moved = pick_two(lane, acc0[high, :] + acc2[high, :], acc1[low, :] + acc3[low, :])
-        field[h] = placed + pltpu.roll(moved, CAPACITY, 1)
-
-    for copy in parent_copies:
-        copy.wait()
+    @pl.when(blocks > 1)
+    def _():
+        near_copy(1).start()
+
     square = (RANK, RANK)
     product = (
         lax.broadcasted_iota(jnp.int32, square, 0) == lax.broadcasted_iota(jnp.int32, square, 1)
     ).astype(F32)
     products = []
     for level in range(LEVELS):
-        parent = parents[level].astype(F32)
+        at = WIDE + level * RANK * LANES // VECTORS
+        parent = jnp.concatenate(
+            [own[:, pl.ds(at + i * LANES, LANES)].astype(F32) for i in range(RANK // VECTORS)],
+            axis=0,
+        )
         own_half = jnp.where(
             ((device >> level) & 1) == 1, pltpu.roll(parent, RANK, 1), parent
         )[:, :RANK]
@@ -442,10 +404,16 @@
         field[MID_AT + h] = pick_two(
             lane, result[16 * h : 16 * h + 8, span], result[16 * h + 8 : 16 * h + 16, span]
         )
-    field_out = pltpu.make_async_copy(field, field_hbm, out_sem.at[0])
-    field_out.start()
+    @pl.when(blocks > 2)
+    def _():
+        near_copy(2).start()
 
     copies[9].wait()
+
+    @pl.when(blocks > 3)
+    def _():
+        near_copy(3).start()
+
     level = lax.broadcasted_iota(jnp.int32, (VECTORS, LANES), 0) + 1
     column = BOXES - lax.shift_right_logical(jnp.full_like(level, BOXES), level - 1)
     column = column + lax.shift_right_logical(jnp.full_like(level, 1) * device, level)
@@ -475,6 +443,44 @@
         coupling[k + 1] = dot_nn(products[k], chosen.astype(BF16)).astype(BF16)
     coupling_out = pltpu.make_async_copy(coupling, coupling_hbm, out_sem.at[1])
     coupling_out.start()
+    zeros_half = jnp.zeros((2 * VECTORS, LANES), BF16)
+
+    def near_step(k, carry):
+        near_copy(k).wait()
+        sources = [near_from.at[2 * k + i] for i in range(2)]
+        targets = [near_to.at[2 * k + i] for i in range(2)]
+        for i in range(BLOCK // 16):
+            rows, weights = [], []
+            for g in range(4):
+                first = 16 * i + 4 * g
+                at = [rows_of(sources[first // LANES][first % LANES + j]) for j in range(4)]
+                top = jnp.concatenate([x_low[at[0], :], x_high[at[1], :]], axis=0)
+                bottom = jnp.concatenate([x_low[at[2], :], x_high[at[3], :]], axis=0)
+                rows.append(jnp.concatenate([top.astype(BF16), zeros_half], axis=1))
+                rows.append(jnp.concatenate([zeros_half, bottom.astype(BF16)], axis=1))
+                weights.append(near[k, :, first * CAPACITY : (first + 4) * CAPACITY])
+            result = dot_nt(jnp.concatenate(rows, axis=0), jnp.concatenate(weights, axis=0))
+            for g in range(4):
+                first = 16 * i + 4 * g
+                for j in range(4):
+                    to = rows_of(targets[first // LANES][first % LANES + j])
+                    at = 32 * g + 8 * j
+                    accumulators[g][to, :] += result[
+                        at : at + 8, (g // 2) * LANES : (g // 2 + 1) * LANES
+                    ]
+        return carry
+
+    lax.fori_loop(0, blocks, near_step, 0)
+    for h in range(LEAVES // 2):
+        low = rows_of(2 * h * VECTORS)
+        high = rows_of((2 * h + 1) * VECTORS)
+        placed = pick_two(lane, acc0[low, :] + acc2[low, :], acc1[high, :] + acc3[high, :])
+        moved = pick_two(lane, acc0[high, :] + acc2[high, :], acc1[low, :] + acc3[low, :])
+        field[h] = placed + pltpu.roll(moved, CAPACITY, 1)
+
+    field_out = pltpu.make_async_copy(field, field_hbm, out_sem.at[0])
+    field_out.start()
+
     field_out.wait()
     coupling_out.wait()
 
@@ -493,6 +499,7 @@
     leaf_transfer,
     basis,
     sem,
+    top_sem,
     pairs0,
     pairs1,
     pairs2,
@@ -500,21 +507,21 @@
     pairs4,
     pairs5,
 ):
-    half = pl.ds(0, BOXES // 2)
-    rest = pl.ds(BOXES // 2, BOXES // 2 - 4)
+    pieces = [
+        pltpu.make_async_copy(
+            top_hbm.at[pl.ds(first, min(8, BOXES - 4 - first))],
+            top_transfer.at[pl.ds(first, min(8, BOXES - 4 - first))],
+            top_sem.at[first // 8],
+        )
+        for first in range(0, BOXES - 4, 8)
+    ]
     copies = [
         pltpu.make_async_copy(source, target, sem.at[i])
         for i, (source, target) in enumerate(
-            (
-                (top_hbm.at[half], top_transfer.at[half]),
-                (top_hbm.at[rest], top_transfer.at[rest]),
-                (mid_hbm, mid_transfer),
-                (leaf_hbm, leaf_transfer),
-                (basis_hbm, basis),
-            )
+            ((mid_hbm, mid_transfer), (leaf_hbm, leaf_transfer), (basis_hbm, basis))
         )
     ]
-    for copy in copies:
+    for copy in pieces + copies:
         copy.start()
     device = lax.axis_index("clusters")
     lane = lane_index((VECTORS, LANES))
@@ -530,11 +537,10 @@
         tile = every[p].astype(F32)
         pairs0[p + 1] = jnp.where(kept, tile, pltpu.roll(pltpu.roll(tile, RANK, 1), 4, 0))
     for level in range(LEVELS):
-        if level < 2:
-            copies[level].wait()
         start = BOXES - (BOXES >> level)
         count = BOXES >> (level + 1)
         for g in range(0, count, 8):
+            pieces[(start + g) // 8].wait()
             left, right = [], []
             for quad in range(g, min(g + 8, count), 4):
                 low = jnp.concatenate([pairs[level][1 + quad], pairs[level][2 + quad]], axis=0)
@@ -560,9 +566,9 @@
         stacked = jnp.concatenate([pick_two(lane, before, middle), after[:, :64]], axis=1)
         down = down + dot_nt(stacked.astype(BF16), coupling[level])
 
-    copies[2].wait()
+    copies[0].wait()
     mid_push = dot_nn(down.astype(BF16), mid_transfer[0])
-    copies[3].wait()
+    copies[1].wait()
     rows = []
     for c in range(GROUPS):
         h = c // 2
@@ -575,7 +581,7 @@
         jnp.concatenate(rows, axis=0).astype(BF16),
         leaf_transfer[...].reshape(GROUPS * RANK, CHILDREN * RANK_LEAF),
     )
-    copies[4].wait()
+    copies[2].wait()
     lane_group = lane // RANK_LEAF
     for first in range(0, LEAVES // 4, 8):
         rows, weights = [], []
@@ -609,7 +615,7 @@
         out_shape=(
             shape((VECTORS, WIDE), BF16),
             shape((BOXES // 2, VECTORS, LANES), BF16),
-            shape((LEVELS, RANK, 2 * RANK), BF16),
+            shape((VECTORS, LOCAL), BF16),
         ),
         in_specs=[hbm] * 5,
         out_specs=(hbm, hbm, hbm),
@@ -621,6 +627,7 @@
             scratch((VECTORS, LEAF_LANES + MID_LANES), BF16),
             scratch((MESSAGES, VECTORS, LANES), BF16),
             scratch((LEVELS, RANK, 2 * RANK), BF16),
+            scratch((VECTORS, LOCAL), BF16),
             dma((4,)),
             dma((2 + BOXES // 2 // MESSAGES,)),
             dma((LEVELS + 1,)),
@@ -637,13 +644,12 @@
     near_count,
     far_source,
     mid_source,
-    packed,
+    local,
     packed_pair,
     packed_other,
     far_coupling,
     mid_coupling,
     top_coupling,
-    parents,
     box_coupling,
     near_blocks,
 ):
@@ -664,15 +670,14 @@
             shape((FIELDS, VECTORS, LANES), F32),
             shape((LEVELS + 1, RANK, 3 * RANK), BF16),
         ),
-        in_specs=[hbm] * 8 + [pl.BlockSpec(memory_space=pltpu.VMEM)] * 2 + [hbm] * 4,
+        in_specs=[hbm] * 8 + [pl.BlockSpec(memory_space=pltpu.VMEM)] * 2 + [hbm] * 3,
         out_specs=(hbm, hbm),
         scratch_shapes=[scratch(i, jnp.int32) for i in indices]
         + [
-            wide,
+            scratch((VECTORS, LOCAL), BF16),
             wide,
             wide,
             scratch((RANK, 3 * RANK, BOXES - 4), BF16),
-            scratch((LEVELS, RANK, 2 * RANK), BF16),
             scratch((1, RANK, 3 * RANK), BF16),
             scratch((PARTS, CAPACITY, PART), BF16),
             scratch((FIELDS, VECTORS, LANES), F32),
@@ -691,7 +696,7 @@
         + [scratch(i, jnp.int32) for i in indices]
         + [pltpu.SMEM((1, 1), jnp.int32)]
         + [pltpu.SMEM(i, jnp.int32) for i in indices]
-        + [dma((PARTS,)), dma((10,)), dma, dma((4,)), dma((2,))],
+        + [dma((PARTS,)), dma((10,)), dma((4,)), dma((2,))],
         cost_estimate=pl.CostEstimate(flops=2 * 10**9, bytes_accessed=10**7, transcendentals=0),
         compiler_params=pltpu.CompilerParams(vmem_limit_bytes=SIDE_LIMIT),
         name="side",
@@ -701,14 +706,13 @@
         near_count.reshape(1, 1),
         far_source.T,
         mid_source,
-        packed,
+        local,
         packed_pair,
         packed_other,
         far_coupling,
         mid_coupling,
         jnp.transpose(top_coupling, (1, 2, 0)),
-        parents,
-        box_coupling,
+            box_coupling,
         near_blocks,
     )
 
@@ -727,7 +731,8 @@
             scratch((1, RANK, GROUPS * RANK), BF16),
             scratch((GROUPS, RANK, CHILDREN * RANK_LEAF), BF16),
             scratch((RANK_LEAF, POINTS), BF16),
-            dma((5,)),
+            dma((3,)),
+            dma((BOXES // 8,)),
         ]
         + [
             scratch(((BOXES >> (level + 1)) + 2, VECTORS, LANES), F32)
@@ -758,7 +763,7 @@
 ):
     pair = [(i, i ^ 1) for i in range(BOXES)]
     other = [(i, min(max(((i + 1) ^ 1) - 1, 0), BOXES - 1)) for i in range(BOXES)]
-    packed, message, parents = up_call(
+    packed, message, local = up_call(
         charges, leaf_basis, leaf_transfer, mid_transfer, top_transfer
     )
     packed_other = lax.ppermute(packed, "clusters", other)
@@ -770,13 +775,12 @@
         near_count,
         far_source,
         mid_source,
-        packed,
+        local,
         packed_pair,
         packed_other,
         far_coupling,
         mid_coupling,
         top_coupling,
-        parents,
         box_coupling,
         near_blocks,
     )

time: 32.1 us -> 33.4 us (1.040)
  the two profiles are of different devices: /device:TPU:127 before, /device:TPU:1 now
where the time goes in v4:
time: 33.4 us; the launch traced here: 33.2 us
  Pallas kernels  15.2 us (46%)
  starting transfers between devices  14.8 us (44%)
  waiting for transfers between devices  1.5 us (4%)
  local copies, waits for them, and re-layouts  0.95 us (3%)
  between operations  0.8 us (2%)
    all_to_all x1, starting transfers between devices, body(): lax.all_to_all(message.reshape(BOXES, VECTORS // 2, LANES), 'clusters', 0...  10.2 us
    pallas_call x1, Pallas kernels, side_call(): pl.pallas_call(side_kernel, out_shape=(shape((FIELDS, VECTORS, LANES), F3...  6.84 us
    pallas_call x1, Pallas kernels, down_call(): pl.pallas_call(down_kernel, out_shape=shape((VECTORS, POINTS), BF16), in_...  5.62 us
    ppermute x1, starting transfers between devices, body(): packed_other = lax.ppermute(packed, 'clusters', other)  4.49 us
    pallas_call x1, Pallas kernels, up_call(): pl.pallas_call(up_kernel, out_shape=(shape((VECTORS, WIDE), BF16), shape(...  2.7 us
    all_to_all x1, waiting for transfers between devices, body(): lax.all_to_all(message.reshape(BOXES, VECTORS // 2, LANES), 'clusters', 0...  1.49 us
    unnamed x18, local copies, waits for them, and re-layouts  0.95 us
  transfers between devices with their start and end apart: 3, of which 1 were waited for; matrix products, arithmetic and copies ran while one was open for 0% of the time, Pallas kernels for 21%

profile of v4, /device:TPU:1, one launch (start us, length us, event | category | flops | bytes accessed | tf_op | source)
XLA Modules:
  0.0 33.2 jit_solution(8494643425900694787)
XLA Ops:
  0.0 0.0 copy-start.5
  0.0 0.0 copy-start.6
  0.0 0.0 copy-start.3
  0.0 0.0 copy-start.1
  0.0 0.0 copy-start.7
  0.0 0.0 copy-start
  0.0 0.0 copy-start.4
  0.0 2.7 %upward.1 = (bf16[8,6656]{1,0:T(8,128)(2,1)}, bf16[64,8,128]{2,1,0:T(8,128)(2,1)}, bf16[8,11776]{1,0:T(8,128)(2,1)}) custom-call(bf16[8,4096]{1,0:T(8,128)(2,1)} %charges_hbm.1, bf16[32,4096]{1,0:T(8,128)(2,1)} %basis_hbm.3, bf16[8,64,256]{2,1,0:T(8,128)(2,1)} %leaf_hbm.3, bf16[1,64,512]{2,1,0:T(8,128)(2,1)} %mid_hbm.3, bf16[124,64,128]{2,1,0:T(8,128)(2,1)} %top_hbm.3), custom_call_target="tpu_custom_call" | custom-call | flops 1000000000 | bytes 1000000 | tf_op jit(solution)/shard_map/upward/pallas_call | solution.py:613
  2.8 4.5 %collective-permute-start.1 = (bf16[8,6656]{1,0:T(8,128)(2,1)}, bf16[8,6656]{1,0:T(8,128)(2,1)S(1)}, u32[]{:S(2)}, u32[]{:S(2)}) collective-permute-start(bf16[8,6656]{1,0:T(8,128)(2,1)} %get-tuple-element.12), channel_id=1, source_target_pairs={{0,0},{1,2},{2,1},{3,4},{4,3},{5,6},{6,5},{7,8},{8,7},{9,10},{10,9... | collective-permute-start | bytes 319496 | tf_op jit(solution)/shard_map/ppermute | solution.py:769
  7.3 0.1 collective-permute-start
  7.4 10.2 %all-to-all-start = ((bf16[128,4,128]{2,1,0:T(4,128)(2,1)}), bf16[128,4,128]{2,1,0:T(4,128)(2,1)S(1)}, u32[]{:S(2)}, u32[]{:S(2)}) async-start(bf16[128,4,128]{2,1,0:T(4,128)(2,1)} %bitcast.13), calls=%async_computation | async-start | bytes 262144 | tf_op jit(solution)/shard_map/all_to_all | solution.py:771
  18.2 0.0 collective-permute-done.1.other_hbm
  18.2 0.0 collective-permute-done.pair_hbm
  18.2 0.0 copy-done.5
  18.2 0.0 copy-done.6
  18.2 0.0 copy-done.3
  18.3 0.0 copy-done.1
  18.3 0.0 copy-done.7
  18.3 0.0 copy-done
  18.3 0.0 copy-done.4
  18.3 0.0 copy-start.2
  18.3 0.9 %copy-done.2 = bf16[8,11776]{1,0:T(8,128)(2,1)S(1)} copy-done((bf16[8,11776]{1,0:T(8,128)(2,1)S(1)}, bf16[8,11776]{1,0:T(8,128)(2,1)}, u32[]{:S(2)}) %copy-start.2) | copy-done | bytes 188440
  19.2 0.0 copy-start.8
  19.2 6.8 %side.1 = (f32[52,8,128]{2,1,0:T(8,128)S(1)}, bf16[6,64,192]{2,1,0:T(8,128)(2,1)S(1)}) custom-call(s32[8,128]{1,0:T(8,128)S(1)} %bitcast.10, s32[8,128]{1,0:T(8,128)S(1)} %bitcast.11, s32[1,1]{1,0:T(1,128)} %bitcast.7.near_count_hbm, s32[16,64]{1,0:T(8,128)S(1)} %bitcast.9, s32[8,8]{1,0:T(8,128)S(1)} %copy-done.7, bf16[8,11776]{1,0:T(8,128)(2,1)S(1)} %copy-done.2, ...), custom_call_target="tpu_custom_call" | custom-call | flops 2000000000 | bytes 10000000 | tf_op jit(solution)/shard_map/side/pallas_call | solution.py:667
  26.1 1.5 %all-to-all-done = bf16[128,4,128]{2,1,0:T(4,128)(2,1)S(1)} async-done(((bf16[128,4,128]{2,1,0:T(4,128)(2,1)}), bf16[128,4,128]{2,1,0:T(4,128)(2,1)S(1)}, u32[]{:S(2)}, u32[]{:S(2)}) %all-to-all-start) | async-done | bytes 131104 | tf_op jit(solution)/shard_map/all_to_all | solution.py:771
  27.6 0.0 copy-done.8
  27.6 5.6 %down.1 = bf16[8,4096]{1,0:T(8,128)(2,1)} custom-call(bf16[64,8,128]{2,1,0:T(8,128)(2,1)S(1)} %bitcast.8, bf16[124,64,128]{2,1,0:T(8,128)(2,1)} %top_hbm.3, bf16[6,64,192]{2,1,0:T(8,128)(2,1)S(1)} %get-tuple-element.13.coupling, bf16[1,64,512]{2,1,0:T(8,128)(2,1)S(1)} %copy-done.8, bf16[8,64,256]{2,1,0:T(8,128)(2,1)} %leaf_hbm.3, ...), custom_call_target="tpu_custom_call" | custom-call | flops 1000000000 | bytes 1000000 | tf_op jit(solution)/shard_map/down/pallas_call | solution.py:724
Async XLA Ops:
  0.0 18.2 %copy-start.5 = (s32[1024]{0:T(1024)S(1)}, s32[1024]{0:T(1024)}, u32[]{:S(2)}) copy-start(s32[1024]{0:T(1024)} %param.27) | copy-start | bytes 12292
  0.0 18.2 %copy-start.6 = (s32[1024]{0:T(1024)S(1)}, s32[1024]{0:T(1024)}, u32[]{:S(2)}) copy-start(s32[1024]{0:T(1024)} %param.26) | copy-start | bytes 12292
  0.0 18.2 %copy-start.3 = (bf16[1,64,192]{2,1,0:T(8,128)(2,1)S(1)}, bf16[1,64,192]{2,1,0:T(8,128)(2,1)}, u32[]{:S(2)}) copy-start(bf16[1,64,192]{2,1,0:T(8,128)(2,1)} %box_coupling_hbm.1) | copy-start | bytes 73732
  0.0 18.3 %copy-start.1 = (bf16[8,64,512]{2,1,0:T(8,128)(2,1)S(1)}, bf16[8,64,512]{2,1,0:T(8,128)(2,1)}, u32[]{:S(2)}) copy-start(bf16[8,64,512]{2,1,0:T(8,128)(2,1)} %mid_coupling.1) | copy-start | bytes 1572868
  0.0 18.3 %copy-start.7 = (s32[8,8]{1,0:T(8,128)S(1)}, s32[8,8]{1,0:T(8,128)}, u32[]{:S(2)}) copy-start(s32[8,8]{1,0:T(8,128)} %mid_source_hbm.1) | copy-start | bytes 772
  0.0 18.3 %copy-start = (bf16[64,32,512]{2,1,0:T(8,128)(2,1)S(1)}, bf16[64,32,512]{2,1,0:T(8,128)(2,1)}, u32[]{:S(2)}) copy-start(bf16[64,32,512]{2,1,0:T(8,128)(2,1)} %far.1) | copy-start | bytes 6291460
  0.0 18.3 %copy-start.4 = (s32[64,16]{0,1:T(8,128)S(1)}, s32[64,16]{0,1:T(8,128)}, u32[]{:S(2)}) copy-start(s32[64,16]{0,1:T(8,128)} %param.19) | copy-start | bytes 12292
  2.8 15.4 %collective-permute-start.1 = (bf16[8,6656]{1,0:T(8,128)(2,1)}, bf16[8,6656]{1,0:T(8,128)(2,1)S(1)}, u32[]{:S(2)}, u32[]{:S(2)}) collective-permute-start(bf16[8,6656]{1,0:T(8,128)(2,1)} %get-tuple-element.12), channel_id=1, source_target_pairs={{0,0},{1,2},{2,1},{3,4},{4,3},{5,6},{6,5},{7,8},{8,7},{9,10},{10,9... | collective-permute-start | bytes 319496 | tf_op jit(solution)/shard_map/ppermute | solution.py:769
  7.3 11.0 %collective-permute-start = (bf16[8,6656]{1,0:T(8,128)(2,1)}, bf16[8,6656]{1,0:T(8,128)(2,1)S(1)}, u32[]{:S(2)}, u32[]{:S(2)}) collective-permute-start(bf16[8,6656]{1,0:T(8,128)(2,1)} %get-tuple-element.12), channel_id=1, source_target_pairs={{0,1},{1,0},{2,3},{3,2},{4,5},{5,4},{6,7},{7,6},{8,9},{9,8},{10,11... | collective-permute-start | bytes 319496 | tf_op jit(solution)/shard_map/ppermute | solution.py:770
  7.4 20.2 %all-to-all-start = ((bf16[128,4,128]{2,1,0:T(4,128)(2,1)}), bf16[128,4,128]{2,1,0:T(4,128)(2,1)S(1)}, u32[]{:S(2)}, u32[]{:S(2)}) async-start(bf16[128,4,128]{2,1,0:T(4,128)(2,1)} %bitcast.13), calls=%async_computation | async-start | bytes 262144 | tf_op jit(solution)/shard_map/all_to_all | solution.py:771
  18.3 0.9 %copy-start.2 = (bf16[8,11776]{1,0:T(8,128)(2,1)S(1)}, bf16[8,11776]{1,0:T(8,128)(2,1)}, u32[]{:S(2)}) copy-start(bf16[8,11776]{1,0:T(8,128)(2,1)} %get-tuple-element.11.own_hbm) | copy-start | bytes 565252
  19.2 8.4 %copy-start.8 = (bf16[1,64,512]{2,1,0:T(8,128)(2,1)S(1)}, bf16[1,64,512]{2,1,0:T(8,128)(2,1)}, u32[]{:S(2)}) copy-start(bf16[1,64,512]{2,1,0:T(8,128)(2,1)} %mid_hbm.3) | copy-start | bytes 196612

commit v5 on v4

--- a/solution.py
+++ b/solution.py
@@ -124,6 +124,13 @@
     )
     charges_out.start()
     copies[1].wait()
+    for copy in parent_copies:
+        copy.wait()
+    local[:, pl.ds(0, POINTS)] = charges[...]
+    for level in range(LEVELS):
+        for i in range(RANK // VECTORS):
+            at = WIDE + (level * (RANK // VECTORS) + i) * LANES
+            local[:, pl.ds(at, LANES)] = parents[level, i * VECTORS : (i + 1) * VECTORS, :]
     tiles = []
     for first in range(0, LEAVES // 4, 8):
         rows, weights = [], []
@@ -158,14 +165,7 @@
         coefficients, packed_hbm.at[:, pl.ds(POINTS, LEAF_LANES + MID_LANES)], out_sem.at[1]
     )
     coefficients_out.start()
-    for copy in parent_copies:
-        copy.wait()
-    local[:, pl.ds(0, POINTS)] = charges[...]
     local[:, pl.ds(POINTS, LEAF_LANES + MID_LANES)] = coefficients[...]
-    for level in range(LEVELS):
-        for i in range(RANK // VECTORS):
-            at = WIDE + (level * (RANK // VECTORS) + i) * LANES
-            local[:, pl.ds(at, LANES)] = parents[level, i * VECTORS : (i + 1) * VECTORS, :]
     local_out = pltpu.make_async_copy(local, local_hbm, parent_sem.at[LEVELS])
     local_out.start()
     copies[3].wait()
@@ -499,7 +499,6 @@
     leaf_transfer,
     basis,
     sem,
-    top_sem,
     pairs0,
     pairs1,
     pairs2,
@@ -507,21 +506,21 @@
     pairs4,
     pairs5,
 ):
-    pieces = [
-        pltpu.make_async_copy(
-            top_hbm.at[pl.ds(first, min(8, BOXES - 4 - first))],
-            top_transfer.at[pl.ds(first, min(8, BOXES - 4 - first))],
-            top_sem.at[first // 8],
-        )
-        for first in range(0, BOXES - 4, 8)
-    ]
+    half = pl.ds(0, BOXES // 2)
+    rest = pl.ds(BOXES // 2, BOXES // 2 - 4)
     copies = [
         pltpu.make_async_copy(source, target, sem.at[i])
         for i, (source, target) in enumerate(
-            ((mid_hbm, mid_transfer), (leaf_hbm, leaf_transfer), (basis_hbm, basis))
+            (
+                (mid_hbm, mid_transfer),
+                (leaf_hbm, leaf_transfer),
+                (basis_hbm, basis),
+                (top_hbm.at[half], top_transfer.at[half]),
+                (top_hbm.at[rest], top_transfer.at[rest]),
+            )
         )
     ]
-    for copy in pieces + copies:
+    for copy in copies[3:] + copies[:3]:
         copy.start()
     device = lax.axis_index("clusters")
     lane = lane_index((VECTORS, LANES))
@@ -537,10 +536,11 @@
         tile = every[p].astype(F32)
         pairs0[p + 1] = jnp.where(kept, tile, pltpu.roll(pltpu.roll(tile, RANK, 1), 4, 0))
     for level in range(LEVELS):
+        if level < 2:
+            copies[3 + level].wait()
         start = BOXES - (BOXES >> level)
         count = BOXES >> (level + 1)
         for g in range(0, count, 8):
-            pieces[(start + g) // 8].wait()
             left, right = [], []
             for quad in range(g, min(g + 8, count), 4):
                 low = jnp.concatenate([pairs[level][1 + quad], pairs[level][2 + quad]], axis=0)
@@ -731,8 +731,7 @@
             scratch((1, RANK, GROUPS * RANK), BF16),
             scratch((GROUPS, RANK, CHILDREN * RANK_LEAF), BF16),
             scratch((RANK_LEAF, POINTS), BF16),
-            dma((3,)),
-            dma((BOXES // 8,)),
+            dma((5,)),
         ]
         + [
             scratch(((BOXES >> (level + 1)) + 2, VECTORS, LANES), F32)

time: 33.4 us -> 31.6 us (0.946)
  Pallas kernels: 15.2 us -> 13.3 us
    pallas_call x1, Pallas kernels: 5.62 us -> 3.79 us  [down_call(): pl.pallas_call(down_kernel, out_shape=shape((VECTORS, POINTS), BF16), in_...]
  transfers between devices with their start and end apart: 3 -> 3, of which waited for: 1 -> 1; matrix products, arithmetic and copies ran while one was open for 0% -> 0% of each run, Pallas kernels for 21% -> 22%
where the time goes in v5:
time: 31.6 us; the launch traced here: 31.4 us
  starting transfers between devices  14.8 us (47%)
  Pallas kernels  13.3 us (42%)
  waiting for transfers between devices  1.5 us (5%)
  local copies, waits for them, and re-layouts  0.95 us (3%)
  between operations  0.8 us (3%)
    all_to_all x1, starting transfers between devices, body(): lax.all_to_all(message.reshape(BOXES, VECTORS // 2, LANES), 'clusters', 0...  10.2 us
    pallas_call x1, Pallas kernels, side_call(): pl.pallas_call(side_kernel, out_shape=(shape((FIELDS, VECTORS, LANES), F3...  6.84 us
    ppermute x1, starting transfers between devices, body(): packed_other = lax.ppermute(packed, 'clusters', other)  4.49 us
    pallas_call x1, Pallas kernels, down_call(): pl.pallas_call(down_kernel, out_shape=shape((VECTORS, POINTS), BF16), in_...  3.79 us
    pallas_call x1, Pallas kernels, up_call(): pl.pallas_call(up_kernel, out_shape=(shape((VECTORS, WIDE), BF16), shape(...  2.7 us
    all_to_all x1, waiting for transfers between devices, body(): lax.all_to_all(message.reshape(BOXES, VECTORS // 2, LANES), 'clusters', 0...  1.5 us
    unnamed x18, local copies, waits for them, and re-layouts  0.95 us
  transfers between devices with their start and end apart: 3, of which 1 were waited for; matrix products, arithmetic and copies ran while one was open for 0% of the time, Pallas kernels for 22%

profile of v5, /device:TPU:1, one launch (start us, length us, event | category | flops | bytes accessed | tf_op | source)
XLA Modules:
  0.0 31.4 jit_solution(7951786795092975186)
XLA Ops:
  0.0 0.0 copy-start.5
  0.0 0.0 copy-start.6
  0.0 0.0 copy-start.3
  0.0 0.0 copy-start.1
  0.0 0.0 copy-start.7
  0.0 0.0 copy-start
  0.0 0.0 copy-start.4
  0.0 2.7 %upward.1 = (bf16[8,6656]{1,0:T(8,128)(2,1)}, bf16[64,8,128]{2,1,0:T(8,128)(2,1)}, bf16[8,11776]{1,0:T(8,128)(2,1)}) custom-call(bf16[8,4096]{1,0:T(8,128)(2,1)} %charges_hbm.1, bf16[32,4096]{1,0:T(8,128)(2,1)} %basis_hbm.3, bf16[8,64,256]{2,1,0:T(8,128)(2,1)} %leaf_hbm.3, bf16[1,64,512]{2,1,0:T(8,128)(2,1)} %mid_hbm.3, bf16[124,64,128]{2,1,0:T(8,128)(2,1)} %top_hbm.3), custom_call_target="tpu_custom_call" | custom-call | flops 1000000000 | bytes 1000000 | tf_op jit(solution)/shard_map/upward/pallas_call | solution.py:613
  2.8 4.5 %collective-permute-start.1 = (bf16[8,6656]{1,0:T(8,128)(2,1)}, bf16[8,6656]{1,0:T(8,128)(2,1)S(1)}, u32[]{:S(2)}, u32[]{:S(2)}) collective-permute-start(bf16[8,6656]{1,0:T(8,128)(2,1)} %get-tuple-element.12), channel_id=1, source_target_pairs={{0,0},{1,2},{2,1},{3,4},{4,3},{5,6},{6,5},{7,8},{8,7},{9,10},{10,9... | collective-permute-start | bytes 319496 | tf_op jit(solution)/shard_map/ppermute | solution.py:768
  7.3 0.1 collective-permute-start
  7.4 10.2 %all-to-all-start = ((bf16[128,4,128]{2,1,0:T(4,128)(2,1)}), bf16[128,4,128]{2,1,0:T(4,128)(2,1)S(1)}, u32[]{:S(2)}, u32[]{:S(2)}) async-start(bf16[128,4,128]{2,1,0:T(4,128)(2,1)} %bitcast.13), calls=%async_computation | async-start | bytes 262144 | tf_op jit(solution)/shard_map/all_to_all | solution.py:770
  18.2 0.0 collective-permute-done.1.other_hbm
  18.2 0.0 collective-permute-done.pair_hbm
  18.2 0.0 copy-done.5
  18.2 0.0 copy-done.6
  18.2 0.0 copy-done.3
  18.3 0.0 copy-done.1
  18.3 0.0 copy-done.7
  18.3 0.0 copy-done
  18.3 0.0 copy-done.4
  18.3 0.0 copy-start.2
  18.3 0.9 %copy-done.2 = bf16[8,11776]{1,0:T(8,128)(2,1)S(1)} copy-done((bf16[8,11776]{1,0:T(8,128)(2,1)S(1)}, bf16[8,11776]{1,0:T(8,128)(2,1)}, u32[]{:S(2)}) %copy-start.2) | copy-done | bytes 188440
  19.2 0.0 copy-start.8
  19.2 6.8 %side.1 = (f32[52,8,128]{2,1,0:T(8,128)S(1)}, bf16[6,64,192]{2,1,0:T(8,128)(2,1)S(1)}) custom-call(s32[8,128]{1,0:T(8,128)S(1)} %bitcast.10, s32[8,128]{1,0:T(8,128)S(1)} %bitcast.11, s32[1,1]{1,0:T(1,128)} %bitcast.7.near_count_hbm, s32[16,64]{1,0:T(8,128)S(1)} %bitcast.9, s32[8,8]{1,0:T(8,128)S(1)} %copy-done.7, bf16[8,11776]{1,0:T(8,128)(2,1)S(1)} %copy-done.2, ...), custom_call_target="tpu_custom_call" | custom-call | flops 2000000000 | bytes 10000000 | tf_op jit(solution)/shard_map/side/pallas_call | solution.py:667
  26.1 1.5 %all-to-all-done = bf16[128,4,128]{2,1,0:T(4,128)(2,1)S(1)} async-done(((bf16[128,4,128]{2,1,0:T(4,128)(2,1)}), bf16[128,4,128]{2,1,0:T(4,128)(2,1)S(1)}, u32[]{:S(2)}, u32[]{:S(2)}) %all-to-all-start) | async-done | bytes 131104 | tf_op jit(solution)/shard_map/all_to_all | solution.py:770
  27.6 0.0 copy-done.8
  27.6 3.8 %down.1 = bf16[8,4096]{1,0:T(8,128)(2,1)} custom-call(bf16[64,8,128]{2,1,0:T(8,128)(2,1)S(1)} %bitcast.8, bf16[124,64,128]{2,1,0:T(8,128)(2,1)} %top_hbm.3, bf16[6,64,192]{2,1,0:T(8,128)(2,1)S(1)} %get-tuple-element.13.coupling, bf16[1,64,512]{2,1,0:T(8,128)(2,1)S(1)} %copy-done.8, bf16[8,64,256]{2,1,0:T(8,128)(2,1)} %leaf_hbm.3, ...), custom_call_target="tpu_custom_call" | custom-call | flops 1000000000 | bytes 1000000 | tf_op jit(solution)/shard_map/down/pallas_call | solution.py:724
Async XLA Ops:
  0.0 18.2 %copy-start.5 = (s32[1024]{0:T(1024)S(1)}, s32[1024]{0:T(1024)}, u32[]{:S(2)}) copy-start(s32[1024]{0:T(1024)} %param.27) | copy-start | bytes 12292
  0.0 18.2 %copy-start.6 = (s32[1024]{0:T(1024)S(1)}, s32[1024]{0:T(1024)}, u32[]{:S(2)}) copy-start(s32[1024]{0:T(1024)} %param.26) | copy-start | bytes 12292
  0.0 18.2 %copy-start.3 = (bf16[1,64,192]{2,1,0:T(8,128)(2,1)S(1)}, bf16[1,64,192]{2,1,0:T(8,128)(2,1)}, u32[]{:S(2)}) copy-start(bf16[1,64,192]{2,1,0:T(8,128)(2,1)} %box_coupling_hbm.1) | copy-start | bytes 73732
  0.0 18.2 %copy-start.1 = (bf16[8,64,512]{2,1,0:T(8,128)(2,1)S(1)}, bf16[8,64,512]{2,1,0:T(8,128)(2,1)}, u32[]{:S(2)}) copy-start(bf16[8,64,512]{2,1,0:T(8,128)(2,1)} %mid_coupling.1) | copy-start | bytes 1572868
  0.0 18.2 %copy-start.7 = (s32[8,8]{1,0:T(8,128)S(1)}, s32[8,8]{1,0:T(8,128)}, u32[]{:S(2)}) copy-start(s32[8,8]{1,0:T(8,128)} %mid_source_hbm.1) | copy-start | bytes 772
  0.0 18.2 %copy-start = (bf16[64,32,512]{2,1,0:T(8,128)(2,1)S(1)}, bf16[64,32,512]{2,1,0:T(8,128)(2,1)}, u32[]{:S(2)}) copy-start(bf16[64,32,512]{2,1,0:T(8,128)(2,1)} %far.1) | copy-start | bytes 6291460
  0.0 18.2 %copy-start.4 = (s32[64,16]{0,1:T(8,128)S(1)}, s32[64,16]{0,1:T(8,128)}, u32[]{:S(2)}) copy-start(s32[64,16]{0,1:T(8,128)} %param.19) | copy-start | bytes 12292
  2.8 15.4 %collective-permute-start.1 = (bf16[8,6656]{1,0:T(8,128)(2,1)}, bf16[8,6656]{1,0:T(8,128)(2,1)S(1)}, u32[]{:S(2)}, u32[]{:S(2)}) collective-permute-start(bf16[8,6656]{1,0:T(8,128)(2,1)} %get-tuple-element.12), channel_id=1, source_target_pairs={{0,0},{1,2},{2,1},{3,4},{4,3},{5,6},{6,5},{7,8},{8,7},{9,10},{10,9... | collective-permute-start | bytes 319496 | tf_op jit(solution)/shard_map/ppermute | solution.py:768
  7.3 11.0 %collective-permute-start = (bf16[8,6656]{1,0:T(8,128)(2,1)}, bf16[8,6656]{1,0:T(8,128)(2,1)S(1)}, u32[]{:S(2)}, u32[]{:S(2)}) collective-permute-start(bf16[8,6656]{1,0:T(8,128)(2,1)} %get-tuple-element.12), channel_id=1, source_target_pairs={{0,1},{1,0},{2,3},{3,2},{4,5},{5,4},{6,7},{7,6},{8,9},{9,8},{10,11... | collective-permute-start | bytes 319496 | tf_op jit(solution)/shard_map/ppermute | solution.py:769
  7.4 20.2 %all-to-all-start = ((bf16[128,4,128]{2,1,0:T(4,128)(2,1)}), bf16[128,4,128]{2,1,0:T(4,128)(2,1)S(1)}, u32[]{:S(2)}, u32[]{:S(2)}) async-start(bf16[128,4,128]{2,1,0:T(4,128)(2,1)} %bitcast.13), calls=%async_computation | async-start | bytes 262144 | tf_op jit(solution)/shard_map/all_to_all | solution.py:770
  18.3 0.9 %copy-start.2 = (bf16[8,11776]{1,0:T(8,128)(2,1)S(1)}, bf16[8,11776]{1,0:T(8,128)(2,1)}, u32[]{:S(2)}) copy-start(bf16[8,11776]{1,0:T(8,128)(2,1)} %get-tuple-element.11.own_hbm) | copy-start | bytes 565252
  19.2 8.4 %copy-start.8 = (bf16[1,64,512]{2,1,0:T(8,128)(2,1)S(1)}, bf16[1,64,512]{2,1,0:T(8,128)(2,1)}, u32[]{:S(2)}) copy-start(bf16[1,64,512]{2,1,0:T(8,128)(2,1)} %mid_hbm.3) | copy-start | bytes 196612

commit v6 on v5

--- a/solution.py
+++ b/solution.py
@@ -506,7 +506,8 @@
     pairs4,
     pairs5,
 ):
-    half = pl.ds(0, BOXES // 2)
+    quarter = pl.ds(0, BOXES // 4)
+    half = pl.ds(BOXES // 4, BOXES // 4)
     rest = pl.ds(BOXES // 2, BOXES // 2 - 4)
     copies = [
         pltpu.make_async_copy(source, target, sem.at[i])
@@ -515,6 +516,7 @@
                 (mid_hbm, mid_transfer),
                 (leaf_hbm, leaf_transfer),
                 (basis_hbm, basis),
+                (top_hbm.at[quarter], top_transfer.at[quarter]),
                 (top_hbm.at[half], top_transfer.at[half]),
                 (top_hbm.at[rest], top_transfer.at[rest]),
             )
@@ -536,11 +538,13 @@
         tile = every[p].astype(F32)
         pairs0[p + 1] = jnp.where(kept, tile, pltpu.roll(pltpu.roll(tile, RANK, 1), 4, 0))
     for level in range(LEVELS):
-        if level < 2:
-            copies[3 + level].wait()
+        if level == 1:
+            copies[5].wait()
         start = BOXES - (BOXES >> level)
         count = BOXES >> (level + 1)
         for g in range(0, count, 8):
+            if level == 0 and g % (BOXES // 4) == 0:
+                copies[3 + g // (BOXES // 4)].wait()
             left, right = [], []
             for quad in range(g, min(g + 8, count), 4):
                 low = jnp.concatenate([pairs[level][1 + quad], pairs[level][2 + quad]], axis=0)
@@ -731,7 +735,7 @@
             scratch((1, RANK, GROUPS * RANK), BF16),
             scratch((GROUPS, RANK, CHILDREN * RANK_LEAF), BF16),
             scratch((RANK_LEAF, POINTS), BF16),
-            dma((5,)),
+            dma((6,)),
         ]
         + [
             scratch(((BOXES >> (level + 1)) + 2, VECTORS, LANES), F32)

time: 31.6 us -> 31.6 us (level)
  no operation moved by 1% of the time
where the time goes in v6:
time: 31.6 us; the launch traced here: 31.3 us
  starting transfers between devices  14.8 us (47%)
  Pallas kernels  13.3 us (42%)
  waiting for transfers between devices  1.5 us (5%)
  local copies, waits for them, and re-layouts  0.95 us (3%)
  between operations  0.8 us (3%)
    all_to_all x1, starting transfers between devices, body(): lax.all_to_all(message.reshape(BOXES, VECTORS // 2, LANES), 'clusters', 0...  10.2 us
    pallas_call x1, Pallas kernels, side_call(): pl.pallas_call(side_kernel, out_shape=(shape((FIELDS, VECTORS, LANES), F3...  6.84 us
    ppermute x1, starting transfers between devices, body(): packed_other = lax.ppermute(packed, 'clusters', other)  4.49 us
    pallas_call x1, Pallas kernels, down_call(): pl.pallas_call(down_kernel, out_shape=shape((VECTORS, POINTS), BF16), in_...  3.75 us
    pallas_call x1, Pallas kernels, up_call(): pl.pallas_call(up_kernel, out_shape=(shape((VECTORS, WIDE), BF16), shape(...  2.7 us
    all_to_all x1, waiting for transfers between devices, body(): lax.all_to_all(message.reshape(BOXES, VECTORS // 2, LANES), 'clusters', 0...  1.5 us
    unnamed x18, local copies, waits for them, and re-layouts  0.95 us
  transfers between devices with their start and end apart: 3, of which 1 were waited for; matrix products, arithmetic and copies ran while one was open for 0% of the time, Pallas kernels for 22%

profile of v6, /device:TPU:1, one launch (start us, length us, event | category | flops | bytes accessed | tf_op | source)
XLA Modules:
  0.0 31.3 jit_solution(591498748877437670)
XLA Ops:
  0.0 0.0 copy-start.5
  0.0 0.0 copy-start.6
  0.0 0.0 copy-start.3
  0.0 0.0 copy-start.1
  0.0 0.0 copy-start.7
  0.0 0.0 copy-start
  0.0 0.0 copy-start.4
  0.0 2.7 %upward.1 = (bf16[8,6656]{1,0:T(8,128)(2,1)}, bf16[64,8,128]{2,1,0:T(8,128)(2,1)}, bf16[8,11776]{1,0:T(8,128)(2,1)}) custom-call(bf16[8,4096]{1,0:T(8,128)(2,1)} %charges_hbm.1, bf16[32,4096]{1,0:T(8,128)(2,1)} %basis_hbm.3, bf16[8,64,256]{2,1,0:T(8,128)(2,1)} %leaf_hbm.3, bf16[1,64,512]{2,1,0:T(8,128)(2,1)} %mid_hbm.3, bf16[124,64,128]{2,1,0:T(8,128)(2,1)} %top_hbm.3), custom_call_target="tpu_custom_call" | custom-call | flops 1000000000 | bytes 1000000 | tf_op jit(solution)/shard_map/upward/pallas_call | solution.py:617
  2.8 4.5 %collective-permute-start.1 = (bf16[8,6656]{1,0:T(8,128)(2,1)}, bf16[8,6656]{1,0:T(8,128)(2,1)S(1)}, u32[]{:S(2)}, u32[]{:S(2)}) collective-permute-start(bf16[8,6656]{1,0:T(8,128)(2,1)} %get-tuple-element.12), channel_id=1, source_target_pairs={{0,0},{1,2},{2,1},{3,4},{4,3},{5,6},{6,5},{7,8},{8,7},{9,10},{10,9... | collective-permute-start | bytes 319496 | tf_op jit(solution)/shard_map/ppermute | solution.py:772
  7.3 0.1 collective-permute-start
  7.4 10.2 %all-to-all-start = ((bf16[128,4,128]{2,1,0:T(4,128)(2,1)}), bf16[128,4,128]{2,1,0:T(4,128)(2,1)S(1)}, u32[]{:S(2)}, u32[]{:S(2)}) async-start(bf16[128,4,128]{2,1,0:T(4,128)(2,1)} %bitcast.13), calls=%async_computation | async-start | bytes 262144 | tf_op jit(solution)/shard_map/all_to_all | solution.py:774
  18.2 0.0 collective-permute-done.1.other_hbm
  18.2 0.0 collective-permute-done.pair_hbm
  18.2 0.0 copy-done.5
  18.2 0.0 copy-done.6
  18.2 0.0 copy-done.3
  18.3 0.0 copy-done.1
  18.3 0.0 copy-done.7
  18.3 0.0 copy-done
  18.3 0.0 copy-done.4
  18.3 0.0 copy-start.2
  18.3 0.9 %copy-done.2 = bf16[8,11776]{1,0:T(8,128)(2,1)S(1)} copy-done((bf16[8,11776]{1,0:T(8,128)(2,1)S(1)}, bf16[8,11776]{1,0:T(8,128)(2,1)}, u32[]{:S(2)}) %copy-start.2) | copy-done | bytes 188440
  19.2 0.0 copy-start.8
  19.2 6.8 %side.1 = (f32[52,8,128]{2,1,0:T(8,128)S(1)}, bf16[6,64,192]{2,1,0:T(8,128)(2,1)S(1)}) custom-call(s32[8,128]{1,0:T(8,128)S(1)} %bitcast.10, s32[8,128]{1,0:T(8,128)S(1)} %bitcast.11, s32[1,1]{1,0:T(1,128)} %bitcast.7.near_count_hbm, s32[16,64]{1,0:T(8,128)S(1)} %bitcast.9, s32[8,8]{1,0:T(8,128)S(1)} %copy-done.7, bf16[8,11776]{1,0:T(8,128)(2,1)S(1)} %copy-done.2, ...), custom_call_target="tpu_custom_call" | custom-call | flops 2000000000 | bytes 10000000 | tf_op jit(solution)/shard_map/side/pallas_call | solution.py:671
  26.1 1.5 %all-to-all-done = bf16[128,4,128]{2,1,0:T(4,128)(2,1)S(1)} async-done(((bf16[128,4,128]{2,1,0:T(4,128)(2,1)}), bf16[128,4,128]{2,1,0:T(4,128)(2,1)S(1)}, u32[]{:S(2)}, u32[]{:S(2)}) %all-to-all-start) | async-done | bytes 131104 | tf_op jit(solution)/shard_map/all_to_all | solution.py:774
  27.6 0.0 copy-done.8
  27.6 3.7 %down.1 = bf16[8,4096]{1,0:T(8,128)(2,1)} custom-call(bf16[64,8,128]{2,1,0:T(8,128)(2,1)S(1)} %bitcast.8, bf16[124,64,128]{2,1,0:T(8,128)(2,1)} %top_hbm.3, bf16[6,64,192]{2,1,0:T(8,128)(2,1)S(1)} %get-tuple-element.13.coupling, bf16[1,64,512]{2,1,0:T(8,128)(2,1)S(1)} %copy-done.8, bf16[8,64,256]{2,1,0:T(8,128)(2,1)} %leaf_hbm.3, ...), custom_call_target="tpu_custom_call" | custom-call | flops 1000000000 | bytes 1000000 | tf_op jit(solution)/shard_map/down/pallas_call | solution.py:728
Async XLA Ops:
  0.0 18.2 %copy-start.5 = (s32[1024]{0:T(1024)S(1)}, s32[1024]{0:T(1024)}, u32[]{:S(2)}) copy-start(s32[1024]{0:T(1024)} %param.27) | copy-start | bytes 12292
  0.0 18.2 %copy-start.6 = (s32[1024]{0:T(1024)S(1)}, s32[1024]{0:T(1024)}, u32[]{:S(2)}) copy-start(s32[1024]{0:T(1024)} %param.26) | copy-start | bytes 12292
  0.0 18.2 %copy-start.3 = (bf16[1,64,192]{2,1,0:T(8,128)(2,1)S(1)}, bf16[1,64,192]{2,1,0:T(8,128)(2,1)}, u32[]{:S(2)}) copy-start(bf16[1,64,192]{2,1,0:T(8,128)(2,1)} %box_coupling_hbm.1) | copy-start | bytes 73732
  0.0 18.2 %copy-start.1 = (bf16[8,64,512]{2,1,0:T(8,128)(2,1)S(1)}, bf16[8,64,512]{2,1,0:T(8,128)(2,1)}, u32[]{:S(2)}) copy-start(bf16[8,64,512]{2,1,0:T(8,128)(2,1)} %mid_coupling.1) | copy-start | bytes 1572868
  0.0 18.2 %copy-start.7 = (s32[8,8]{1,0:T(8,128)S(1)}, s32[8,8]{1,0:T(8,128)}, u32[]{:S(2)}) copy-start(s32[8,8]{1,0:T(8,128)} %mid_source_hbm.1) | copy-start | bytes 772
  0.0 18.2 %copy-start = (bf16[64,32,512]{2,1,0:T(8,128)(2,1)S(1)}, bf16[64,32,512]{2,1,0:T(8,128)(2,1)}, u32[]{:S(2)}) copy-start(bf16[64,32,512]{2,1,0:T(8,128)(2,1)} %far.1) | copy-start | bytes 6291460
  0.0 18.2 %copy-start.4 = (s32[64,16]{0,1:T(8,128)S(1)}, s32[64,16]{0,1:T(8,128)}, u32[]{:S(2)}) copy-start(s32[64,16]{0,1:T(8,128)} %param.19) | copy-start | bytes 12292
  2.8 15.4 %collective-permute-start.1 = (bf16[8,6656]{1,0:T(8,128)(2,1)}, bf16[8,6656]{1,0:T(8,128)(2,1)S(1)}, u32[]{:S(2)}, u32[]{:S(2)}) collective-permute-start(bf16[8,6656]{1,0:T(8,128)(2,1)} %get-tuple-element.12), channel_id=1, source_target_pairs={{0,0},{1,2},{2,1},{3,4},{4,3},{5,6},{6,5},{7,8},{8,7},{9,10},{10,9... | collective-permute-start | bytes 319496 | tf_op jit(solution)/shard_map/ppermute | solution.py:772
  7.3 11.0 %collective-permute-start = (bf16[8,6656]{1,0:T(8,128)(2,1)}, bf16[8,6656]{1,0:T(8,128)(2,1)S(1)}, u32[]{:S(2)}, u32[]{:S(2)}) collective-permute-start(bf16[8,6656]{1,0:T(8,128)(2,1)} %get-tuple-element.12), channel_id=1, source_target_pairs={{0,1},{1,0},{2,3},{3,2},{4,5},{5,4},{6,7},{7,6},{8,9},{9,8},{10,11... | collective-permute-start | bytes 319496 | tf_op jit(solution)/shard_map/ppermute | solution.py:773
  7.4 20.2 %all-to-all-start = ((bf16[128,4,128]{2,1,0:T(4,128)(2,1)}), bf16[128,4,128]{2,1,0:T(4,128)(2,1)S(1)}, u32[]{:S(2)}, u32[]{:S(2)}) async-start(bf16[128,4,128]{2,1,0:T(4,128)(2,1)} %bitcast.13), calls=%async_computation | async-start | bytes 262144 | tf_op jit(solution)/shard_map/all_to_all | solution.py:774
  18.3 0.9 %copy-start.2 = (bf16[8,11776]{1,0:T(8,128)(2,1)S(1)}, bf16[8,11776]{1,0:T(8,128)(2,1)}, u32[]{:S(2)}) copy-start(bf16[8,11776]{1,0:T(8,128)(2,1)} %get-tuple-element.11.own_hbm) | copy-start | bytes 565252
  19.2 8.4 %copy-start.8 = (bf16[1,64,512]{2,1,0:T(8,128)(2,1)S(1)}, bf16[1,64,512]{2,1,0:T(8,128)(2,1)}, u32[]{:S(2)}) copy-start(bf16[1,64,512]{2,1,0:T(8,128)(2,1)} %mid_hbm.3) | copy-start | bytes 196612
